TPU v7x, 128 devices: a whole 4x4x4 slice. The times are simulated.
128 devices in a mesh: rep: 2 (over core), dp: 64 (over x, y, z).
Axes of the slice: x: 4, y: 4, z: 4, core: 2. Of those that a mesh axis runs over, the one named last changes fastest.
Arguments:
- x: bfloat16 [128, 1024, 1536], P(('rep', 'dp')), parts along dimension 0
- dy: bfloat16 [128, 1024, 1536], P(('rep', 'dp')), parts along dimension 0
- w_gate: bfloat16 [2, 1536, 4096], replicated
- w_up: bfloat16 [2, 1536, 4096], replicated
- w_down: bfloat16 [2, 4096, 1536], replicated
- m_w_gate: float32 [2, 1536, 4096], P(None, 'dp')
- m_w_up: float32 [2, 1536, 4096], P(None, 'dp')
- m_w_down: float32 [2, 4096, 1536], P(None, 'dp')
- v_w_gate: float32 [2, 1536, 4096], P(None, 'dp')
- v_w_up: float32 [2, 1536, 4096], P(None, 'dp')
- v_w_down: float32 [2, 4096, 1536], P(None, 'dp')
Outputs:
- output 1: bfloat16 [4, 1536, 4096], P('rep'), parts along dimension 0
- output 2: bfloat16 [4, 1536, 4096], P('rep'), parts along dimension 0
- output 3: bfloat16 [4, 4096, 1536], P('rep'), parts along dimension 0
- output 4: float32 [4, 1536, 4096], P('rep', 'dp'), parts along dimension 0
- output 5: float32 [4, 1536, 4096], P('rep', 'dp'), parts along dimension 0
- output 6: float32 [4, 4096, 1536], P('rep', 'dp'), parts along dimension 0
- output 7: float32 [4, 1536, 4096], P('rep', 'dp'), parts along dimension 0
- output 8: float32 [4, 1536, 4096], P('rep', 'dp'), parts along dimension 0
- output 9: float32 [4, 4096, 1536], P('rep', 'dp'), parts along dimension 0
There are 2 independent parts. A program takes and returns all parts, laid end to end along the dimension named above; an argument that names none is the same for every part.
All inputs are finite; a program needn't handle non-finite values.
Results may differ from a plain program's by a relative error of at most 0.022.
Values are sent between devices in bfloat16 or wider.
A program may use at most 1.5 GiB of HBM per device.

v0:
```python
import jax
import jax.numpy as jnp
from jax import lax

NAMES = ("w_gate", "w_up", "w_down")


def matmul(a, w):
    return jnp.dot(a, w, preferred_element_type=jnp.float32).astype(jnp.bfloat16)


def normed(h):
    wide = h.astype(jnp.float32)
    scale = lax.rsqrt(jnp.mean(wide**2, -1, keepdims=True) + 1e-6)
    return (wide * scale).astype(jnp.bfloat16)


def layer(h, w):
    a = normed(h)
    gate = jnp.dot(a, w["w_gate"], preferred_element_type=jnp.float32)
    up = jnp.dot(a, w["w_up"], preferred_element_type=jnp.float32)
    return h + matmul((jax.nn.silu(gate) * up).astype(jnp.bfloat16), w["w_down"])


def adamw(w, m, v, g):
    m = 0.9 * m + 0.1 * g
    v = 0.95 * v + 0.05 * g * g
    step = m * lax.rsqrt(v + 1e-8) + 0.1 * w
    return (w - 0.02 * step).astype(jnp.bfloat16), m, v


def stack(weights, h):
    for number in range(weights["w_gate"].shape[0]):
        h = layer(h, {name: w[number] for name, w in weights.items()})
    return h


def solution(mesh):
    groups = mesh.shape["rep"]

    def step(x, dy, *arrays):
        weights, m, v = (arrays[i : i + 3] for i in (0, 3, 6))
        x, dy = (t.reshape(groups, -1, *t.shape[1:]) for t in (x, dy))

        def of_a_group(x, dy):
            _, back = jax.vjp(lambda w: stack(w, x), dict(zip(NAMES, weights, strict=True)))
            by_weights = back(dy)[0]
            gradients = [by_weights[name].astype(jnp.float32) for name in NAMES]
            new = [adamw(w.astype(jnp.float32), m, v, g) for w, m, v, g in zip(weights, m, v, gradients, strict=True)]
            return tuple(one[which] for which in range(3) for one in new)

        return tuple(t.reshape(-1, *t.shape[2:]) for t in jax.vmap(of_a_group)(x, dy))

    return step
```

profile of v0, /device:TPU:0, one launch (start us, length us, event | category | flops | bytes accessed | tf_op | source)
XLA Modules:
  0.0 2191.7 jit_solution(12243279238119705467)
XLA Ops:
  9.8 20.5 fusion.36
  30.3 19.6 fusion.34
  81.8 19.9 fusion.22
  101.7 19.8 fusion.26
  140.0 25.2 %fusion.78 = bf16[1024,1536]{1,0:T(8,128)(2,1)} fusion(bf16[2,1536,4096]{2,1,0:T(8,128)(2,1)} %param, f32[1024,4096]{1,0:T(8,128)} %fusion.22, f32[1024,4096]{1,0:T(8,128)} %fusion.26, bf16[1024,4096]{1,0:T(8,128)(2,1)} %fusion.60), kind=kOutput, calls=%fused_computation.90 | convolution fusion | flops 12932612096 | bytes 57671680 | tf_op jit(solution)/vmap(transpose(jvp()))/dot_general | solution.py:20
  165.2 24.4 %fusion.69 = (f32[1024]{0:T(1024)S(1)}, bf16[1024,1536]{1,0:T(8,128)(2,1)}) fusion(bf16[1,1,1024,1536]{3,2,1,0:T(8,128)(2,1)} %copy-done.16, bf16[1024,1536]{1,0:T(8,128)(2,1)} %fusion.78, bf16[2,1536,4096]{2,1,0:T(8,128)(2,1)} %param.3, bf16[1024,4096]{1,0:T(8,128)(2,1)} %fusion.60, f32[1024,4096]{1,0:T(8,128)} %fusion.22), kind=kOutput, calls=%fused_computation.86 | convolution fusion | flops 12919503872 | bytes 47190016 | tf_op jit(solution)/vmap(transpose(jvp()))/dot_general | solution.py:21
  189.6 25.1 %convolution_bitcast_fusion = f32[1,4096,1536]{2,1,0:T(8,128)} fusion(bf16[1024,4096]{1,0:T(8,128)(2,1)} %copy-done, bf16[1,1,1024,1536]{3,2,1,0:T(8,128)(2,1)} %copy-done.16, bf16[1024,1536]{1,0:T(8,128)(2,1)} %get-tuple-element.12, bf16[1,1024,1536]{2,1,0:T(8,128)(2,1)} %param.5, f32[1024]{0:T(1024)S(1)} %bitcast.350, f32[1024]{0:T(1024)S(1)} %bitcast.355), kind=kOutput, calls=%fused_computation.6 | convolution fusion | flops 12895911936 | bytes 42999808 | tf_op jit(solution)/vmap(transpose(jvp()))/dot_general | solution.py:9
  216.7 27.4 %convolution_bitcast_fusion.1 = f32[1,4096,1536]{2,1,0:T(8,128)} fusion(f32[1024,4096]{1,0:T(8,128)} %fusion.26, f32[1024,4096]{1,0:T(8,128)} %fusion.22, bf16[1,1024,1536]{2,1,0:T(8,128)(2,1)S(1)} %copy-done.14), kind=kOutput, calls=%fused_computation.7 | convolution fusion | flops 12910067712 | bytes 61865984 | tf_op jit(solution)/vmap(transpose(jvp()))/dot_general | solution.py:9
  244.2 21.2 fusion.57
  265.4 30.2 %convolution_bitcast_fusion.4 = f32[1,1536,4096]{2,1,0:T(8,128)} fusion(f32[1024,4096]{1,0:T(8,128)} %fusion.36, f32[1024,4096]{1,0:T(8,128)} %fusion.34, bf16[1024,4096]{1,0:T(8,128)(2,1)} %fusion.57, bf16[1,1024,1536]{2,1,0:T(8,128)(2,1)S(1)} %copy-done.2, f32[1024]{0:T(1024)S(1)} %copy-done.12), kind=kOutput, calls=%fused_computation.10 | convolution fusion | flops 12935757824 | bytes 70258688 | tf_op jit(solution)/vmap(transpose(jvp()))/dot_general | solution.py:20
  295.6 31.3 %convolution_bitcast_fusion.5 = f32[1,1536,4096]{2,1,0:T(8,128)} fusion(bf16[1,1,1024,1536]{3,2,1,0:T(8,128)(2,1)} %copy-done.16, f32[1024]{0:T(1024)S(1)} %bitcast.357, f32[1024,4096]{1,0:T(8,128)} %fusion.22, f32[1024,4096]{1,0:T(8,128)} %fusion.26, bf16[1024,4096]{1,0:T(8,128)(2,1)} %fusion.60), kind=kOutput, calls=%fused_computation.11 | convolution fusion | flops 12935757824 | bytes 70258688 | tf_op jit(solution)/vmap(transpose(jvp()))/dot_general | solution.py:20
  327.0 23.6 %convolution_bitcast_fusion.2 = f32[1,1536,4096]{2,1,0:T(8,128)} fusion(bf16[1024,4096]{1,0:T(8,128)(2,1)} %fusion.57, f32[1024,4096]{1,0:T(8,128)} %fusion.36, bf16[1,1024,1536]{2,1,0:T(8,128)(2,1)S(1)} %copy-done.2, f32[1024]{0:T(1024)S(1)} %copy-done.12), kind=kOutput, calls=%fused_computation.8 | convolution fusion | flops 12914786304 | bytes 53481472 | tf_op jit(solution)/vmap(transpose(jvp()))/dot_general | solution.py:21
  352.5 23.4 %convolution_bitcast_fusion.3 = f32[1,1536,4096]{2,1,0:T(8,128)} fusion(bf16[1024,4096]{1,0:T(8,128)(2,1)} %fusion.60, f32[1024,4096]{1,0:T(8,128)} %fusion.22, bf16[1,1,1024,1536]{3,2,1,0:T(8,128)(2,1)S(1)} %copy-done.17, f32[1024]{0:T(1024)S(1)} %bitcast.358), kind=kOutput, calls=%fused_computation.9 | convolution fusion | flops 12914786304 | bytes 53481472 | tf_op jit(solution)/vmap(transpose(jvp()))/dot_general | solution.py:21
  377.8 89.9 %reduce-scatter.29.cloned.1.call-done = f32[1,64,1536]{2,1,0:T(8,128)} async-done(((f32[1,4096,1536]{2,1,0:T(8,128)}), f32[1,64,1536]{2,1,0:T(8,128)}) %reduce-scatter.29.cloned.1.call-update) | async-done | bytes 393232
  468.7 251.6 %reduce-scatter.27.cloned.1.call-done = f32[1,64,1536]{2,1,0:T(8,128)} async-done(((f32[1,4096,1536]{2,1,0:T(8,128)}), f32[1,64,1536]{2,1,0:T(8,128)}) %reduce-scatter.27.cloned.1.call-update) | async-done | bytes 393232
  724.1 249.3 %reduce-scatter.21.cloned.1.call-done = f32[1,24,4096]{2,1,0:T(8,128)} async-done(((f32[1,1536,4096]{2,1,0:T(8,128)}), f32[1,24,4096]{2,1,0:T(8,128)}) %reduce-scatter.21.cloned.1.call-update) | async-done | bytes 393232
  974.4 251.4 %reduce-scatter.19.cloned.1.call-done = f32[1,24,4096]{2,1,0:T(8,128)} async-done(((f32[1,1536,4096]{2,1,0:T(8,128)}), f32[1,24,4096]{2,1,0:T(8,128)}) %reduce-scatter.19.cloned.1.call-update) | async-done | bytes 393232
  1229.6 249.0 %reduce-scatter.25.cloned.1.call-done = f32[1,24,4096]{2,1,0:T(8,128)} async-done(((f32[1,1536,4096]{2,1,0:T(8,128)}), f32[1,24,4096]{2,1,0:T(8,128)}) %reduce-scatter.25.cloned.1.call-update) | async-done | bytes 393232
  1479.6 251.0 %reduce-scatter.23.cloned.1.call-done = f32[1,24,4096]{2,1,0:T(8,128)} async-done(((f32[1,1536,4096]{2,1,0:T(8,128)}), f32[1,24,4096]{2,1,0:T(8,128)}) %reduce-scatter.23.cloned.1.call-update) | async-done | bytes 393232
  1734.8 127.0 %all-gather.14.cloned.1.call-done = bf16[1,2,4096,1536]{3,2,1,0:T(8,128)(2,1)} async-done(((bf16[1,2,64,1536]{3,2,1,0:T(8,128)(2,1)}), bf16[1,2,4096,1536]{3,2,1,0:T(8,128)(2,1)}) %all-gather.14.cloned.1.call-update) | async-done | bytes 25165840 | tf_op jit(solution)/reshape | solution.py:52
  1861.9 134.0 %all-gather.10.cloned.1.call-done = bf16[1,2,1536,4096]{3,2,1,0:T(8,128)(2,1)} async-done(((bf16[1,2,24,4096]{3,2,1,0:T(8,128)(2,1)}), bf16[1,2,1536,4096]{3,2,1,0:T(8,128)(2,1)}) %all-gather.10.cloned.1.call-update) | async-done | bytes 25165840 | tf_op jit(solution)/reshape | solution.py:52
  1995.8 134.0 %all-gather.12.cloned.1.call-done = bf16[1,2,1536,4096]{3,2,1,0:T(8,128)(2,1)} async-done(((bf16[1,2,24,4096]{3,2,1,0:T(8,128)(2,1)}), bf16[1,2,1536,4096]{3,2,1,0:T(8,128)(2,1)}) %all-gather.12.cloned.1.call-update) | async-done | bytes 25165840 | tf_op jit(solution)/reshape | solution.py:52
  2129.8 23.0 %copy.3 = bf16[2,1536,4096]{2,1,0:T(8,128)(2,1)} copy(bf16[2,1536,4096]{2,1,0:T(8,128)(2,1)} %bitcast.346) | data formatting | bytes 50331648
  2152.8 23.0 %copy.4 = bf16[2,1536,4096]{2,1,0:T(8,128)(2,1)} copy(bf16[2,1536,4096]{2,1,0:T(8,128)(2,1)} %bitcast.347) | data formatting | bytes 50331648
  (86 shorter events, 81.8 us)
Async XLA Ops:
  7.2 460.5 %reduce-scatter.29.cloned.1.call-start = ((), (), s32[]{:S(2)}) async-start(), calls=%async_computation.14 | async-start | bytes 25559040
  81.1 40.4 %copy-start.16 = (bf16[1,1,1024,1536]{3,2,1,0:T(8,128)(2,1)}, bf16[1,1,1024,1536]{3,2,1,0:T(8,128)(2,1)S(1)}, u32[]{:S(2)}) copy-start(bf16[1,1,1024,1536]{3,2,1,0:T(8,128)(2,1)S(1)} %get-tuple-element.10) | copy-start | bytes 9437188
  165.2 24.4 %copy-start.8 = (f32[1024]{0:T(1024)S(1)}, f32[1024]{0:T(1024)}, u32[]{:S(2)}) copy-start(f32[1024]{0:T(1024)} %copy-done.7) | copy-start | bytes 12292
  165.2 24.5 %copy-start.10 = (f32[1,1,1024]{2,1,0:T(1,128)S(1)}, f32[1,1,1024]{2,1,0:T(1,128)}, u32[]{:S(2)}) copy-start(f32[1,1,1024]{2,1,0:T(1,128)} %copy-done.9) | copy-start | bytes 12292
  214.8 505.5 %reduce-scatter.27.cloned.1.call-start = ((), (), s32[]{:S(2)}) async-start(), calls=%async_computation.13 | async-start | bytes 25559040
  244.1 21.3 copy-start.2
  244.1 21.3 copy-start.12
  244.1 729.2 %reduce-scatter.21.cloned.1.call-start = ((), (), s32[]{:S(2)}) async-start(), calls=%async_computation.10 | async-start | bytes 25559040
  295.6 930.2 %reduce-scatter.19.cloned.1.call-start = ((), (), s32[]{:S(2)}) async-start(), calls=%async_computation.9 | async-start | bytes 25559040
  327.0 1151.6 %reduce-scatter.25.cloned.1.call-start = ((), (), s32[]{:S(2)}) async-start(), calls=%async_computation.12 | async-start | bytes 25559040
  350.6 1380.0 %reduce-scatter.23.cloned.1.call-start = ((), (), s32[]{:S(2)}) async-start(), calls=%async_computation.11 | async-start | bytes 25559040
  375.9 345.4 %copy-start.3 = (f32[2,64,1536]{2,1,0:T(8,128)S(1)}, f32[2,64,1536]{2,1,0:T(8,128)}, u32[]{:S(2)}) copy-start(f32[2,64,1536]{2,1,0:T(8,128)} %param.10) | copy-start | bytes 2359300
  375.9 345.4 %copy-start.4 = (f32[2,64,1536]{2,1,0:T(8,128)S(1)}, f32[2,64,1536]{2,1,0:T(8,128)}, u32[]{:S(2)}) copy-start(f32[2,64,1536]{2,1,0:T(8,128)} %param.9) | copy-start | bytes 2359300
  375.9 850.9 %copy-start.5 = (f32[2,24,4096]{2,1,0:T(8,128)S(1)}, f32[2,24,4096]{2,1,0:T(8,128)}, u32[]{:S(2)}) copy-start(f32[2,24,4096]{2,1,0:T(8,128)} %param.6) | copy-start | bytes 2359300
  375.9 850.9 %copy-start.6 = (f32[2,24,4096]{2,1,0:T(8,128)S(1)}, f32[2,24,4096]{2,1,0:T(8,128)}, u32[]{:S(2)}) copy-start(f32[2,24,4096]{2,1,0:T(8,128)} %param.1) | copy-start | bytes 2359300
  375.9 1485.9 %all-gather.14.cloned.1.call-start = ((), (), s32[]{:S(2)}) async-start(), calls=%async_computation.8 | async-start | bytes 25559040 | tf_op jit(solution)/reshape | solution.py:52
  724.0 1271.8 %all-gather.10.cloned.1.call-start = ((), (), s32[]{:S(2)}) async-start(), calls=%async_computation.6 | async-start | bytes 25559040 | tf_op jit(solution)/reshape | solution.py:52
  1229.5 900.3 %all-gather.12.cloned.1.call-start = ((), (), s32[]{:S(2)}) async-start(), calls=%async_computation.7 | async-start | bytes 25559040 | tf_op jit(solution)/reshape | solution.py:52
  2129.8 45.9 %slice-start = ((s8[25165824]{0:T(1024)(128)(4,1)}), s8[4194304]{0:T(1024)(128)(4,1)S(1)}, s32[]{:S(2)}) async-start(s8[25165824]{0:T(1024)(128)(4,1)} %bitcast.343), calls=%async_computation.15 | async-start | bytes 8388608
  2129.8 45.9 %slice-start.1 = ((s8[25165824]{0:T(1024)(128)(4,1)}), s8[4194304]{0:T(1024)(128)(4,1)S(1)}, s32[]{:S(2)}) async-start(s8[25165824]{0:T(1024)(128)(4,1)} %bitcast.343), calls=%async_computation.16 | async-start | bytes 8388608
  2129.8 45.9 %slice-start.2 = ((s8[25165824]{0:T(1024)(128)(4,1)}), s8[4194304]{0:T(1024)(128)(4,1)S(1)}, s32[]{:S(2)}) async-start(s8[25165824]{0:T(1024)(128)(4,1)} %bitcast.343), calls=%async_computation.17 | async-start | bytes 8388608
  2152.8 23.0 %slice-start.3 = ((s8[25165824]{0:T(1024)(128)(4,1)}), s8[4194304]{0:T(1024)(128)(4,1)S(1)}, s32[]{:S(2)}) async-start(s8[25165824]{0:T(1024)(128)(4,1)} %bitcast.343), calls=%async_computation.18 | async-start | bytes 8388608
  2152.8 23.0 %slice-start.4 = ((s8[25165824]{0:T(1024)(128)(4,1)}), s8[4194304]{0:T(1024)(128)(4,1)S(1)}, s32[]{:S(2)}) async-start(s8[25165824]{0:T(1024)(128)(4,1)} %bitcast.343), calls=%async_computation.19 | async-start | bytes 8388608
  2152.8 23.0 %slice-start.5 = ((s8[25165824]{0:T(1024)(128)(4,1)}), s8[4194304]{0:T(1024)(128)(4,1)S(1)}, s32[]{:S(2)}) async-start(s8[25165824]{0:T(1024)(128)(4,1)} %bitcast.343), calls=%async_computation.20 | async-start | bytes 8388608
  (9 other events, 104.9 us)
Sparse Core Ops, SparseCore 0:
  214.9 252.6 reduce-scatter.28
  472.4 247.8 reduce-scatter.26
  725.6 247.7 reduce-scatter.20
  978.5 247.2 reduce-scatter.18
  1230.9 247.6 reduce-scatter.24
  1483.2 247.4 reduce-scatter.22
  1733.4 128.4 all-gather.13
  1865.2 130.5 all-gather.9
  1999.2 130.5 all-gather.11
where the time goes:
time: 2200 us; the launch traced here: 2190 us
  waiting for transfers between devices  1740 us (79%)
  matrix products  349 us (16%)
  local copies, waits for them, and re-layouts  60.3 us (3%)
  other arithmetic  29.3 us (1%)
    unnamed x15, waiting for transfers between devices  1340 us
    reshape x3, waiting for transfers between devices, step(): t.reshape(-1, *t.shape[2:])  395 us
    dot_general x5, matrix products, layer(): gate = jnp.dot(a, w['w_gate'], preferred_element_type=jnp.float32)  127 us
    dot_general x5, matrix products, matmul(): jnp.dot(a, w, preferred_element_type=jnp.float32).astype(jnp.bfloat16)  111 us
    dot_general x5, matrix products, layer(): up = jnp.dot(a, w['w_up'], preferred_element_type=jnp.float32)  111 us
    unnamed x51, local copies, waits for them, and re-layouts  59.7 us
  transfers between devices with their start and end apart: 9, of which 9 were waited for; matrix products, arithmetic and copies ran while one was open for 8% of the time, Pallas kernels for 0%

commit v1 on v0

v1 whole, which is shorter than its diff:
```python
import functools
import jax, jax.numpy as jnp
from jax import lax
from jax.experimental import pallas as pl
from jax.experimental.pallas import tpu as pltpu
MESH = pl.DeviceIdType.MESH
BF, F32 = jnp.bfloat16, jnp.float32
ORDERS = ((0, 1, 2), (1, 2, 0), (2, 0, 1))
STRIDE = (16, 4, 1)

from jax.sharding import PartitionSpec as P

NAMES = ("w_gate", "w_up", "w_down")
KINDS = ("wide", "wide", "tall")


def place():
    me = lax.axis_index("dp")
    at = (me // 16, (me // 4) % 4, me % 4)
    def step(axis, by):
        return me + (lax.rem(at[axis] + by, 4) - at[axis]) * STRIDE[axis]
    right = [step(a, 1) for a in range(3)]
    left = [step(a, 3) for a in range(3)]
    return at, left, right

def greet(left, right):
    barrier = pltpu.get_barrier_semaphore()
    for to in (*left, *right):
        pl.semaphore_signal(barrier, inc=1, device_id={"dp": to}, device_id_type=MESH)
    pl.semaphore_wait(barrier, 6)

def piece(kind, color, half):
    if kind == "wide":
        cols = slice(None) if half is None else pl.ds(2048 * half, 2048)
        return (pl.ds(8 * color, 8), cols)
    cols = pl.ds(512 * color, 512) if half is None else pl.ds(512 * color + 256 * half, 256)
    return (slice(None), cols)

def gather_kernel(kinds, *refs):
    n = len(kinds)
    own, out = refs[:n], refs[n:2 * n]
    held, (lsem, psem, ssem, rsem) = refs[2 * n:3 * n], refs[3 * n:]
    at, left, right = place()
    loads = [pltpu.make_async_copy(own[m], held[m], lsem.at[m]) for m in range(n)]
    for c in loads: c.start()
    greet(left, right)
    mine = [pltpu.make_async_copy(held[m], out[m].at[at[0], at[1], at[2]], psem.at[m]) for m in range(n)]
    for m in range(n):
        loads[m].wait()
        mine[m].start()
    nxt = [lax.rem(a + 1, 4) for a in at]
    prv = [lax.rem(a + 3, 4) for a in at]

    def where(color, phase, j, half):
        order = ORDERS[color]
        idx = [at[0], at[1], at[2]]
        idx[order[phase]] = j
        for p in range(phase + 1, 3):
            idx[order[p]] = slice(None)
        return tuple(idx)

    def msg(m, color, phase, d, fwd, sending):
        axis = ORDERS[color][phase]
        a = at[axis]
        back, ahead = (prv[axis], nxt[axis]) if d == 0 else (nxt[axis], prv[axis])
        if sending:
            j = back if fwd else a
        else:
            j = lax.rem(a + 2, 4) if fwd else back
        half = d if fwd else None
        dst = out[m].at[(*where(color, phase, j, half), *piece(kinds[m], color, half))]
        src = dst
        if phase == 2 and not fwd:
            src = held[m].at[piece(kinds[m], color, None)]
        to = (right if d == 0 else left)[axis]
        k = (phase * 3 + color) * 4 + d * 2 + int(fwd)
        return pltpu.make_async_remote_copy(src_ref=src, dst_ref=dst, send_sem=ssem.at[m, k], recv_sem=rsem.at[m, k],
            device_id={"dp": to}, device_id_type=MESH)

    for phase in (2, 1, 0):
        for m in range(n):
            if phase == 1: mine[m].wait()
            for color in range(3):
                if phase < 2:
                    for d in (0, 1): msg(m, color, phase + 1, d, True, False).wait_recv()
                for d in (0, 1): msg(m, color, phase, d, False, True).start()
        for m in range(n):
            for color in range(3):
                for d in (0, 1):
                    msg(m, color, phase, d, False, False).wait_recv()
                    msg(m, color, phase, d, True, True).start()
    for m in range(n):
        for color in range(3):
            for d in (0, 1): msg(m, color, 0, d, True, False).wait_recv()
    for m in range(n):
        for phase in range(3):
            for color in range(3):
                for d in (0, 1):
                    for fwd in (False, True): msg(m, color, phase, d, fwd, True).wait_send()

BLOCK = {"wide": (24, 4096), "tall": (64, 1536)}

def gather(kinds, blocks, cid):
    n = len(kinds)
    return pl.pallas_call(
        functools.partial(gather_kernel, kinds),
        out_shape=[jax.ShapeDtypeStruct((4, 4, 4, *BLOCK[k]), BF) for k in kinds],
        in_specs=[pl.BlockSpec(memory_space=pl.ANY)] * n,
        out_specs=[pl.BlockSpec(memory_space=pl.ANY)] * n,
        scratch_shapes=[*(pltpu.VMEM(BLOCK[k], BF) for k in kinds),
            pltpu.SemaphoreType.DMA((n,)), pltpu.SemaphoreType.DMA((n,)),
            pltpu.SemaphoreType.DMA((n, 36)), pltpu.SemaphoreType.DMA((n, 36))],
        compiler_params=pltpu.CompilerParams(collective_id=cid, has_side_effects=True, vmem_limit_bytes=60 << 20),
        name="gather",
    )(*blocks)

PIECE = {"wide": (8, 2048), "tall": (64, 256)}
SLOTS = 4


def scatter_scratch(kinds):
    n, out = len(kinds), {}
    for m, kind in enumerate(kinds):
        p = PIECE[kind]
        for phase, lead in ((1, (3, 2, 4, 4)), (2, (3, 2, 4)), (3, (3, 2))):
            for letter in "ABC":
                out[f"{letter}{phase}", m] = pltpu.VMEM((*lead, *p), BF)
            if phase > 1:
                for letter in "AB":
                    out[f"{letter}s{phase}", m] = pltpu.VMEM((*lead, *p), BF)
                for letter in "CK":
                    out[f"{letter}o{phase}", m] = pltpu.VMEM((*lead, *p), F32)
        out["G", m] = pltpu.VMEM(BLOCK[kind], BF)
    for kind in dict.fromkeys(kinds):
        out["slot", kind] = pltpu.VMEM((SLOTS, 4, 4, *PIECE[kind]), BF)
        out["slot_sem", kind] = pltpu.SemaphoreType.DMA((SLOTS,))
    out["out_sem"] = pltpu.SemaphoreType.DMA((n,))
    out["send"] = pltpu.SemaphoreType.DMA((n, 54))
    out["recv"] = pltpu.SemaphoreType.DMA((n, 54))
    return out


class Scatter:
    def __init__(self, kinds, src, dst, has):
        self.kinds, self.src, self.dst, self.has = kinds, src, dst, has
        self.at, self.left, self.right = place()
        self.by = [[lax.rem(a + o, 4) for a in self.at] for o in range(4)]
        ms = range(len(kinds))
        self.loads = {k: [(m, u, c, d) for u in (0, 1) for m in ms if kinds[m] == k for c in range(3) for d in (0, 1)] for k in kinds}
        self.taken = {k: 0 for k in kinds}

    def ahead(self, d):
        return 1 if d == 0 else 3

    def load(self, kind, i):
        m, use, c, d = self.loads[kind][i]
        axis = ORDERS[c][0]
        idx = [slice(None)] * 3
        idx[axis] = self.by[0 if use else self.ahead(d)][axis]
        return pltpu.make_async_copy(self.src[m].at[(*idx, *piece(kind, c, d))], self.has["slot", kind].at[i % SLOTS],
            self.has["slot_sem", kind].at[i % SLOTS])

    def take(self, m, use, c, d):
        kind = self.kinds[m]
        i = self.taken[kind]
        assert self.loads[kind][i] == (m, use, c, d)
        self.load(kind, i).wait()
        return self.has["slot", kind].at[i % SLOTS]

    def give(self, m):
        kind = self.kinds[m]
        i = self.taken[kind]
        self.taken[kind] += 1
        if i + SLOTS < len(self.loads[kind]):
            self.load(kind, i + SLOTS).start()

    def copy(self, letter, phase, m, c, d):
        axis = ORDERS[c][phase - 1]
        if letter == "C":
            src = self.has[f"A{phase}", m].at[c, d]
        elif phase > 1:
            src = self.has[f"{letter}s{phase}", m].at[c, d]
        else:
            idx = [slice(None)] * 3
            idx[axis] = self.by[2 if letter == "A" else self.ahead(d)][axis]
            src = self.src[m].at[(*idx, *piece(self.kinds[m], c, d if letter == "A" else 1 - d))]
        k = ((phase - 1) * 3 + "ABC".index(letter)) * 6 + c * 2 + d
        return pltpu.make_async_remote_copy(src_ref=src, dst_ref=self.has[f"{letter}{phase}", m].at[c, d],
            send_sem=self.has["send"].at[m, k], recv_sem=self.has["recv"].at[m, k],
            device_id={"dp": (self.right if d == 0 else self.left)[axis]}, device_id_type=MESH)

    def begin(self):
        for kind in self.loads:
            for i in range(SLOTS):
                self.load(kind, i).start()

    def send(self, m):
        for letter in "AB":
            for c in range(3):
                for d in (0, 1):
                    self.copy(letter, 1, m, c, d).start()

    def combine(self, phase, m, c, d):
        self.copy("A", phase, m, c, d).wait_recv()
        a = self.has[f"A{phase}", m].at[c, d]
        if phase == 1:
            own = self.take(m, 0, c, d)

            @pl.loop(0, 16)
            def _(i):
                at = (i // 4, i % 4)
                a[at] = (a[at].astype(F32) + own[at].astype(F32)).astype(BF)

            self.give(m)
        elif phase == 2:
            own = self.has["Co2", m].at[c, d]

            @pl.loop(0, 4)
            def _(i):
                a[i] = (a[i].astype(F32) + own[i]).astype(BF)
        else:
            a[...] = (a[...].astype(F32) + self.has["Co3", m][c, d]).astype(BF)
        self.copy("C", phase, m, c, d).start()

    def roles(self, h):
        return (("As", h, 2), ("Bs", 1 - h, self.ahead(1 - h)), ("Co", h, self.ahead(h)), ("Ko", h, 0))

    def total(self, phase, m, c, h):
        self.copy("C", phase, m, c, h).wait_recv()
        self.copy("B", phase, m, c, 1 - h).wait_recv()
        one, two = self.has[f"C{phase}", m].at[c, h], self.has[f"B{phase}", m].at[c, 1 - h]
        order = ORDERS[c]
        if phase == 1:
            own = self.take(m, 1, c, h)
            for name, d, o in self.roles(h):
                to = self.has[f"{name}2", m].at[c, d]
                t = self.by[o][order[1]]

                @pl.loop(0, 4)
                def _(i):
                    at = (t, i) if order[1] < order[2] else (i, t)
                    to[i] = (own[at].astype(F32) + one[at].astype(F32) + two[at].astype(F32)).astype(to.dtype)

                if name in ("As", "Bs"):
                    self.copy(name[0], 2, m, c, d).start()
            self.give(m)
        elif phase == 2:
            own = self.has["Ko2", m].at[c, h]
            for name, d, o in self.roles(h):
                t = self.by[o][order[2]]
                to = self.has[f"{name}3", m].at[c, d]
                to[...] = (own[t] + one[t].astype(F32) + two[t].astype(F32)).astype(to.dtype)
                if name in ("As", "Bs"):
                    self.copy(name[0], 3, m, c, d).start()
        else:
            whole = self.has["Ko3", m][c, h] + one[...].astype(F32) + two[...].astype(F32)
            self.has["G", m][piece(self.kinds[m], c, h)] = whole.astype(BF)

    def out(self, m):
        return pltpu.make_async_copy(self.has["G", m], self.dst[m], self.has["out_sem"].at[m])

    def steps(self):
        ms = range(len(self.kinds))
        for phase in (1, 2, 3):
            for what in (self.combine, self.total):
                for m in ms:
                    for c in range(3):
                        for d in (0, 1):
                            yield functools.partial(what, phase, m, c, d)
        for m in ms:
            yield lambda m=m: self.out(m).start()

    def end(self):
        for m in range(len(self.kinds)):
            self.out(m).wait()
            for phase in (1, 2, 3):
                for letter in "ABC":
                    for c in range(3):
                        for d in (0, 1):
                            self.copy(letter, phase, m, c, d).wait_send()


def scatter_kernel(kinds, names, *refs):
    n = len(kinds)
    src, dst, has = refs[:n], refs[n:2 * n], dict(zip(names, refs[2 * n:], strict=True))
    it = Scatter(kinds, src, dst, has)
    it.begin()
    greet(it.left, it.right)
    for m in range(n):
        it.send(m)
    for step in it.steps():
        step()
    it.end()


def scatter(kinds, whole, cid):
    n = len(kinds)
    held = scatter_scratch(kinds)
    return pl.pallas_call(
        functools.partial(scatter_kernel, kinds, tuple(held)),
        out_shape=[jax.ShapeDtypeStruct(BLOCK[k], BF) for k in kinds],
        in_specs=[pl.BlockSpec(memory_space=pl.ANY)] * n,
        out_specs=[pl.BlockSpec(memory_space=pl.ANY)] * n,
        scratch_shapes=list(held.values()),
        compiler_params=pltpu.CompilerParams(collective_id=cid, has_side_effects=True, vmem_limit_bytes=63 << 20),
        name="scatter",
    )(*(w.reshape(4, 4, 4, *BLOCK[k]) for w, k in zip(whole, kinds)))


def matmul(a, w):
    return jnp.dot(a, w, preferred_element_type=F32).astype(BF)


def normed(h):
    wide = h.astype(F32)
    scale = lax.rsqrt(jnp.mean(wide**2, -1, keepdims=True) + 1e-6)
    return (wide * scale).astype(BF)


def layer(h, w):
    a = normed(h)
    gate = jnp.dot(a, w[0], preferred_element_type=F32)
    up = jnp.dot(a, w[1], preferred_element_type=F32)
    return h + matmul((jax.nn.silu(gate) * up).astype(BF), w[2])


def adamw(w, m, v, g):
    m = 0.9 * m + 0.1 * g
    v = 0.95 * v + 0.05 * g * g
    step = m * lax.rsqrt(v + 1e-8) + 0.1 * w
    return (w - 0.02 * step).astype(BF), m, v


def solution(mesh):
    def step(x, dy, *arrays):
        weights, m, v = (arrays[i : i + 3] for i in (0, 3, 6))
        me = lax.axis_index("dp")
        layers = weights[0].shape[0]
        h, backs = x[0], []
        for number in range(layers):
            h, back = jax.vjp(layer, h, tuple(w[number] for w in weights))
            backs.append(back)
        by_h, sums = dy[0], [None] * layers
        for number in reversed(range(layers)):
            by_h, by_w = backs[number](by_h)
            sums[number] = by_w
        for number in reversed(range(layers)):
            sums[number] = scatter(KINDS, sums[number], 1)
        new = []
        for i, kind in enumerate(KINDS):
            w = lax.dynamic_slice_in_dim(weights[i], me * BLOCK[kind][0], BLOCK[kind][0], axis=1)
            g = jnp.stack([sums[number][i] for number in range(layers)])
            new.append(adamw(w.astype(F32), m[i], v[i], g.astype(F32)))
        whole = gather(KINDS * layers, [new[i][0][number] for number in range(layers) for i in range(3)], 2)
        out = [jnp.stack([whole[number * 3 + i].reshape(weights[i].shape[1:]) for number in range(layers)]) for i in range(3)]
        return (*out, *(new[i][which] for which in (1, 2) for i in range(3)))

    blocks = P(None, "dp", None)
    return jax.shard_map(step, mesh=mesh, in_specs=(P(("rep", "dp")),) * 2 + (P(),) * 3 + (blocks,) * 6,
        out_specs=(P("rep"),) * 3 + (P("rep", "dp", None),) * 6, check_vma=False)
```

time: 2200 us -> 965 us (0.44)
  waiting for transfers between devices: 1740 us -> 0 us
  Pallas kernels: 0 us -> 558 us
  local copies, waits for them, and re-layouts: 60.3 us -> 4.08 us
  other arithmetic: 29.3 us -> 66.8 us
  matrix products: 349 us -> 326 us
    unnamed x15 -> x0, waiting for transfers between devices: 1340 us -> none
    pallas_call x0 -> x3, Pallas kernels: none -> 558 us  [the longest x2 290 us: scatter(): pl.pallas_call(functools.partial(scatter_kernel, kinds, tuple(held)), out...]
    reshape x3 -> x0, waiting for transfers between devices: 395 us -> none  [step(): t.reshape(-1, *t.shape[2:])]
    unnamed x51 -> x38, local copies, waits for them, and re-layouts: 59.7 us -> 1.73 us
    another operation x0 -> x3, other arithmetic: none -> 51.6 us  [step(): jnp.stack([whole[number * 3 + i].reshape(weights[i].shape[1:]) for number...]
    dot_general x15, matrix products: 349 us -> 326 us  [the longest x5 114 us: layer(): up = jnp.dot(a, w[1], preferred_element_type=F32)]
  transfers between devices with their start and end apart: 9 -> 0, of which waited for: 9 -> 0; matrix products, arithmetic and copies ran while one was open for 8% -> 0% of each run, Pallas kernels for 0% -> 0%
where the time goes in v1:
time: 965 us; the launch traced here: 957 us
  Pallas kernels  558 us (58%)
  matrix products  326 us (34%)
  other arithmetic  66.8 us (7%)
    pallas_call x2, Pallas kernels, scatter(): pl.pallas_call(functools.partial(scatter_kernel, kinds, tuple(held)), out...  290 us
    pallas_call x1, Pallas kernels, gather(): pl.pallas_call(functools.partial(gather_kernel, kinds), out_shape=[jax.Sh...  268 us
    dot_general x5, matrix products, layer(): up = jnp.dot(a, w[1], preferred_element_type=F32)  114 us
    dot_general x5, matrix products, layer(): gate = jnp.dot(a, w[0], preferred_element_type=F32)  113 us
    dot_general x5, matrix products, matmul(): return jnp.dot(a, w, preferred_element_type=F32).astype(BF)  99.5 us
    another operation x3, other arithmetic, step(): jnp.stack([whole[number * 3 + i].reshape(weights[i].shape[1:]) for number...  51.6 us

profile of v1, /device:TPU:0, one launch (start us, length us, event | category | flops | bytes accessed | tf_op | source)
XLA Modules:
  0.0 956.6 jit_solution(12824531365434101738)
XLA Ops:
  3.3 19.4 %fusion.46 = bf16[1024,4096]{1,0:T(8,128)(2,1)} fusion(bf16[2,4096,1536]{2,1,0:T(8,128)(2,1)} %param.15, bf16[1,1024,1536]{2,1,0:T(8,128)(2,1)} %param.12), kind=kOutput, calls=%fused_computation.65 | convolution fusion | flops 12889096192 | bytes 24117248 | tf_op jit(solution)/shard_map/transpose(jvp())/dot_general | solution.py:311
  22.6 19.6 %fusion.31 = f32[1024,4096]{1,0:T(8,128)} fusion(bf16[2,1536,4096]{2,1,0:T(8,128)(2,1)} %param.13, bf16[1,1024,1536]{2,1,0:T(8,128)(2,1)S(1)} %copy-done.1, f32[1024]{0:T(1024)S(1)} %add_rsqrt_fusion), kind=kOutput, calls=%fused_computation.45 | convolution fusion | flops 12889620480 | bytes 32509952 | tf_op jit(solution)/shard_map/jvp()/dot_general | solution.py:322
  42.2 26.4 %multiply_convert_fusion.1 = (bf16[1024,4096]{1,0:T(8,128)(2,1)}, f32[1024,4096]{1,0:T(8,128)}) fusion(f32[1024,4096]{1,0:T(8,128)} %fusion.31, bf16[2,1536,4096]{2,1,0:T(8,128)(2,1)} %param.14, bf16[1,1024,1536]{2,1,0:T(8,128)(2,1)S(1)} %copy-done.1, f32[1024]{0:T(1024)S(1)} %add_rsqrt_fusion), kind=kOutput, calls=%fused_computation.20 | convolution fusion | flops 12914786304 | bytes 57675776 | tf_op jit(solution)/shard_map/jvp()/dot_general | solution.py:323
  68.6 19.0 %fusion.53 = (f32[1024]{0:T(1024)S(1)}, bf16[1024,1536]{1,0:T(8,128)(2,1)S(1)}) fusion(bf16[1024,4096]{1,0:T(8,128)(2,1)} %get-tuple-element.48, bf16[2,4096,1536]{2,1,0:T(8,128)(2,1)} %param.15, bf16[1,1024,1536]{2,1,0:T(8,128)(2,1)S(1)} %copy-done.1), kind=kOutput, calls=%fused_computation.70 | convolution fusion | flops 12892765184 | bytes 27267072 | tf_op jit(solution)/shard_map/jvp()/dot_general | solution.py:311
  89.2 19.6 %fusion.15 = f32[1024,4096]{1,0:T(8,128)} fusion(bf16[2,1536,4096]{2,1,0:T(8,128)(2,1)} %param.14, bf16[1024,1536]{1,0:T(8,128)(2,1)S(1)} %get-tuple-element.51, f32[1024]{0:T(1024)S(1)} %fusion.94), kind=kOutput, calls=%fused_computation.29 | convolution fusion | flops 12889620480 | bytes 32509952 | tf_op jit(solution)/shard_map/jvp()/dot_general | solution.py:323
  108.8 29.4 %fusion.2 = (bf16[1024,4096]{1,0:T(8,128)(2,1)}, f32[1024,4096]{1,0:T(8,128)}) fusion(f32[1024,4096]{1,0:T(8,128)} %fusion.15, bf16[1024,4096]{1,0:T(8,128)(2,1)} %fusion.46, bf16[2,1536,4096]{2,1,0:T(8,128)(2,1)} %param.13, bf16[1024,1536]{1,0:T(8,128)(2,1)} %copy-done.4, f32[1024]{0:T(1024)S(1)} %fusion.94), kind=kOutput, calls=%fused_computation.11 | convolution fusion | flops 12939952128 | bytes 66064384 | tf_op jit(solution)/shard_map/jvp()/dot_general | solution.py:322
  138.3 21.7 %convolution_convert_fusion.2 = bf16[4096,1536]{1,0:T(8,128)(2,1)} fusion(f32[1024,4096]{1,0:T(8,128)} %fusion.15, bf16[1,1024,1536]{2,1,0:T(8,128)(2,1)S(1)} %copy-done.3, f32[1024,4096]{1,0:T(8,128)} %get-tuple-element.53), kind=kOutput, calls=%fused_computation.25 | convolution fusion | flops 12916359168 | bytes 49283072 | tf_op jit(solution)/shard_map/transpose(jvp())/dot_general | solution.py:311
  160.0 19.2 %fusion.62 = bf16[1024,1536]{1,0:T(8,128)(2,1)} fusion(bf16[1024,4096]{1,0:T(8,128)(2,1)} %get-tuple-element.52, bf16[2,1536,4096]{2,1,0:T(8,128)(2,1)} %param.13), kind=kOutput, calls=%fused_computation.76 | convolution fusion | flops 12884901888 | bytes 24117248 | tf_op jit(solution)/shard_map/transpose(jvp())/dot_general | solution.py:322
  179.2 24.6 %fusion.55 = (f32[1024]{0:T(1024)S(1)}, bf16[1024,1536]{1,0:T(8,128)(2,1)}) fusion(bf16[1024,1536]{1,0:T(8,128)(2,1)} %copy-done.4, bf16[1024,1536]{1,0:T(8,128)(2,1)} %fusion.62, bf16[2,1536,4096]{2,1,0:T(8,128)(2,1)} %param.14, bf16[1024,4096]{1,0:T(8,128)(2,1)} %fusion.46, f32[1024,4096]{1,0:T(8,128)} %get-tuple-element.53), kind=kOutput, calls=%fused_computation.72 | convolution fusion | flops 12919503872 | bytes 47190016 | tf_op jit(solution)/shard_map/transpose(jvp())/dot_general | solution.py:323
  203.8 22.4 %convolution_convert_fusion = bf16[1536,4096]{1,0:T(8,128)(2,1)} fusion(bf16[1024,4096]{1,0:T(8,128)(2,1)} %fusion.46, bf16[1024,1536]{1,0:T(8,128)(2,1)} %copy-done.4, f32[1024]{0:T(1024)S(1)} %fusion.94, f32[1024,4096]{1,0:T(8,128)} %get-tuple-element.53), kind=kOutput, calls=%fused_computation.23 | convolution fusion | flops 12921077760 | bytes 40898560 | tf_op jit(solution)/shard_map/transpose(jvp())/dot_general | solution.py:323
  226.2 5.0 fusion.66
  231.2 19.8 %convolution_convert_fusion.1 = bf16[1536,4096]{1,0:T(8,128)(2,1)} fusion(bf16[1024,4096]{1,0:T(8,128)(2,1)} %get-tuple-element.52, bf16[1024,1536]{1,0:T(8,128)(2,1)S(1)} %copy-done.5, f32[1024]{0:T(1024)S(1)} %fusion.94), kind=kOutput, calls=%fused_computation.24 | convolution fusion | flops 12889620480 | bytes 24121344 | tf_op jit(solution)/shard_map/transpose(jvp())/dot_general | solution.py:322
  251.0 147.3 %scatter.3 = (bf16[24,4096]{1,0:T(8,128)(2,1)}, bf16[24,4096]{1,0:T(8,128)(2,1)}, bf16[64,1536]{1,0:T(8,128)(2,1)}) custom-call(bf16[4,4,4,24,4096]{4,3,2,1,0:T(8,128)(2,1)} %bitcast.114, bf16[4,4,4,24,4096]{4,3,2,1,0:T(8,128)(2,1)} %bitcast.101, bf16[4,4,4,64,1536]{4,3,2,1,0:T(8,128)(2,1)} %bitcast.100), custom_call_target="tpu_custom_call" | custom-call | tf_op jit(solution)/shard_map/scatter/pallas_call | solution.py:299
  398.4 20.9 %convolution_convert_fusion.3 = bf16[4096,1536]{1,0:T(8,128)(2,1)} fusion(bf16[1024,4096]{1,0:T(8,128)(2,1)} %get-tuple-element.48, bf16[1024,1536]{1,0:T(8,128)(2,1)} %fusion.66), kind=kOutput, calls=%fused_computation.26 | convolution fusion | flops 12891193344 | bytes 24117248 | tf_op jit(solution)/shard_map/transpose(jvp())/dot_general | solution.py:311
  419.3 18.4 %fusion.43 = bf16[1024,4096]{1,0:T(8,128)(2,1)} fusion(bf16[1024,1536]{1,0:T(8,128)(2,1)S(1)} %copy-done.6, bf16[2,4096,1536]{2,1,0:T(8,128)(2,1)} %param.15), kind=kOutput, calls=%fused_computation.64 | convolution fusion | flops 12889096192 | bytes 24117248 | tf_op jit(solution)/shard_map/transpose(jvp())/dot_general | solution.py:311
  437.7 24.5 %fusion.11 = bf16[1536,4096]{1,0:T(8,128)(2,1)} fusion(f32[1024,4096]{1,0:T(8,128)} %fusion.31, f32[1024,4096]{1,0:T(8,128)} %get-tuple-element.49, bf16[1024,4096]{1,0:T(8,128)(2,1)} %fusion.43, bf16[1,1024,1536]{2,1,0:T(8,128)(2,1)S(1)} %copy-done.2, f32[1024]{0:T(1024)S(1)} %copy-done.12), kind=kOutput, calls=%fused_computation.27 | convolution fusion | flops 12942049280 | bytes 57675776 | tf_op jit(solution)/shard_map/transpose(jvp())/dot_general | solution.py:322
  462.3 21.5 %fusion.14 = bf16[1536,4096]{1,0:T(8,128)(2,1)} fusion(bf16[1024,4096]{1,0:T(8,128)(2,1)} %fusion.43, f32[1024,4096]{1,0:T(8,128)} %fusion.31, bf16[1,1024,1536]{2,1,0:T(8,128)(2,1)S(1)} %copy-done.2, f32[1024]{0:T(1024)S(1)} %copy-done.12), kind=kOutput, calls=%fused_computation.28 | convolution fusion | flops 12921077760 | bytes 40898560 | tf_op jit(solution)/shard_map/transpose(jvp())/dot_general | solution.py:323
  483.7 142.7 %scatter.2 = (bf16[24,4096]{1,0:T(8,128)(2,1)}, bf16[24,4096]{1,0:T(8,128)(2,1)}, bf16[64,1536]{1,0:T(8,128)(2,1)}) custom-call(bf16[4,4,4,24,4096]{4,3,2,1,0:T(8,128)(2,1)} %bitcast.113, bf16[4,4,4,24,4096]{4,3,2,1,0:T(8,128)(2,1)} %bitcast.115, bf16[4,4,4,64,1536]{4,3,2,1,0:T(8,128)(2,1)} %bitcast.110), custom_call_target="tpu_custom_call" | custom-call | tf_op jit(solution)/shard_map/scatter/pallas_call | solution.py:299
  626.4 2.9 fusion.89
  630.1 4.6 fusion.81
  636.3 268.1 %gather.1 = (bf16[4,4,4,24,4096]{4,3,2,1,0:T(8,128)(2,1)}, bf16[4,4,4,24,4096]{4,3,2,1,0:T(8,128)(2,1)}, bf16[4,4,4,64,1536]{4,3,2,1,0:T(8,128)(2,1)}, bf16[4,4,...) custom-call(bf16[24,4096]{1,0:T(8,128)(2,1)} %get-tuple-element.47.refs_0_, ...), custom_call_target="tpu_custom_call" | custom-call | tf_op jit(solution)/shard_map/gather/pallas_call | solution.py:105
  904.5 24.9 %pad_maximum_fusion = bf16[2,1536,4096]{2,1,0:T(8,128)(2,1)} fusion(bf16[1,1536,4096]{2,1,0:T(8,128)(2,1)} %bitcast.112, bf16[1,1536,4096]{2,1,0:T(8,128)(2,1)} %bitcast.111), kind=kLoop, calls=%fused_computation | loop fusion | flops 12582912 | bytes 50331648 | tf_op jit(solution)/shard_map/stack | solution.py:355
  929.4 16.9 %pad_maximum_fusion.1 = bf16[2,1536,4096]{2,1,0:T(8,128)(2,1)} fusion(bf16[1,1536,4096]{2,1,0:T(8,128)(2,1)} %bitcast.109, bf16[1,1536,4096]{2,1,0:T(8,128)(2,1)S(1)} %bitcast.108), kind=kLoop, calls=%fused_computation.1 | loop fusion | flops 12582912 | bytes 50331648 | tf_op jit(solution)/shard_map/stack | solution.py:355
  946.4 9.8 %pad_maximum_fusion.2 = bf16[2,4096,1536]{2,1,0:T(8,128)(2,1)} fusion(bf16[1,4096,1536]{2,1,0:T(8,128)(2,1)S(1)} %bitcast.107, bf16[1,4096,1536]{2,1,0:T(8,128)(2,1)S(1)} %bitcast.104), kind=kLoop, calls=%fused_computation.2 | loop fusion | flops 12582912 | bytes 50331648 | tf_op jit(solution)/shard_map/stack | solution.py:355
  (47 shorter events, 6.7 us)
Async XLA Ops:
  3.2 39.0 %copy-start.11 = (f32[1024]{0:T(1024)}, f32[1024]{0:T(1024)S(1)}, u32[]{:S(2)}) copy-start(f32[1024]{0:T(1024)S(1)} %add_rsqrt_fusion) | copy-start | bytes 12292
  3.2 19.4 %copy-start.1 = (bf16[1,1024,1536]{2,1,0:T(8,128)(2,1)S(1)}, bf16[1,1024,1536]{2,1,0:T(8,128)(2,1)}, u32[]{:S(2)}) copy-start(bf16[1,1024,1536]{2,1,0:T(8,128)(2,1)} %param.11) | copy-start | bytes 9437188
  87.6 1.7 copy-start.4
  87.6 1.7 copy-start.9
  108.8 29.4 %copy-start.3 = (bf16[1,1024,1536]{2,1,0:T(8,128)(2,1)S(1)}, bf16[1,1024,1536]{2,1,0:T(8,128)(2,1)}, u32[]{:S(2)}) copy-start(bf16[1,1024,1536]{2,1,0:T(8,128)(2,1)} %param.12) | copy-start | bytes 9437188
  203.8 22.4 %copy-start.10 = (f32[1024]{0:T(1024)S(1)}, f32[1024]{0:T(1024)}, u32[]{:S(2)}) copy-start(f32[1024]{0:T(1024)} %copy-done.9) | copy-start | bytes 12292
  226.2 5.0 copy-start.5
  398.3 20.9 %copy-start.6 = (bf16[1024,1536]{1,0:T(8,128)(2,1)S(1)}, bf16[1024,1536]{1,0:T(8,128)(2,1)}, u32[]{:S(2)}) copy-start(bf16[1024,1536]{1,0:T(8,128)(2,1)} %fusion.66) | copy-start | bytes 9437188
  419.3 18.5 %copy-start.2 = (bf16[1,1024,1536]{2,1,0:T(8,128)(2,1)S(1)}, bf16[1,1024,1536]{2,1,0:T(8,128)(2,1)}, u32[]{:S(2)}) copy-start(bf16[1,1024,1536]{2,1,0:T(8,128)(2,1)} %param.11) | copy-start | bytes 9437188
  419.3 18.5 %copy-start.12 = (f32[1024]{0:T(1024)S(1)}, f32[1024]{0:T(1024)}, u32[]{:S(2)}) copy-start(f32[1024]{0:T(1024)} %copy-done.11) | copy-start | bytes 12292
  483.7 142.7 %copy-start.7 = (f32[2,64,1536]{2,1,0:T(8,128)S(1)}, f32[2,64,1536]{2,1,0:T(8,128)}, u32[]{:S(2)}) copy-start(f32[2,64,1536]{2,1,0:T(8,128)} %param.21) | copy-start | bytes 2359300
  483.7 142.7 %copy-start.8 = (bf16[64,1536]{1,0:T(8,128)(2,1)S(1)}, bf16[64,1536]{1,0:T(8,128)(2,1)}, u32[]{:S(2)}) copy-start(bf16[64,1536]{1,0:T(8,128)(2,1)} %get-tuple-element.26) | copy-start | bytes 589828
  904.4 25.0 %copy-start = (bf16[4,4,4,24,4096]{4,3,2,1,0:T(8,128)(2,1)S(1)}, bf16[4,4,4,24,4096]{4,3,2,1,0:T(8,128)(2,1)}, u32[]{:S(2)}) copy-start(bf16[4,4,4,24,4096]{4,3,2,1,0:T(8,128)(2,1)} %get-tuple-element.29) | copy-start | bytes 37748740
  904.4 41.9 %slice-start = ((s8[12582912]{0:T(1024)(128)(4,1)}), s8[4194304]{0:T(1024)(128)(4,1)S(1)}, s32[]{:S(2)}) async-start(s8[12582912]{0:T(1024)(128)(4,1)} %bitcast.102), calls=%async_computation | async-start | bytes 8388608
  904.4 41.9 %slice-start.1 = ((s8[12582912]{0:T(1024)(128)(4,1)}), s8[4194304]{0:T(1024)(128)(4,1)S(1)}, s32[]{:S(2)}) async-start(s8[12582912]{0:T(1024)(128)(4,1)} %bitcast.102), calls=%async_computation.1 | async-start | bytes 8388608
  904.5 41.9 %slice-start.3 = ((s8[12582912]{0:T(1024)(128)(4,1)}), s8[4194304]{0:T(1024)(128)(4,1)S(1)}, s32[]{:S(2)}) async-start(s8[12582912]{0:T(1024)(128)(4,1)} %bitcast.105), calls=%async_computation.3 | async-start | bytes 8388608
  904.5 41.9 %slice-start.4 = ((s8[12582912]{0:T(1024)(128)(4,1)}), s8[4194304]{0:T(1024)(128)(4,1)S(1)}, s32[]{:S(2)}) async-start(s8[12582912]{0:T(1024)(128)(4,1)} %bitcast.105), calls=%async_computation.4 | async-start | bytes 8388608
  929.4 17.0 %slice-start.2 = ((s8[12582912]{0:T(1024)(128)(4,1)}), s8[4194304]{0:T(1024)(128)(4,1)S(1)}, s32[]{:S(2)}) async-start(s8[12582912]{0:T(1024)(128)(4,1)} %bitcast.102), calls=%async_computation.2 | async-start | bytes 8388608
  929.4 17.0 %slice-start.5 = ((s8[12582912]{0:T(1024)(128)(4,1)}), s8[4194304]{0:T(1024)(128)(4,1)S(1)}, s32[]{:S(2)}) async-start(s8[12582912]{0:T(1024)(128)(4,1)} %bitcast.105), calls=%async_computation.5 | async-start | bytes 8388608

commit v2 on v1

--- a/solution.py
+++ b/solution.py
@@ -110,21 +110,25 @@
         scratch_shapes=[*(pltpu.VMEM(BLOCK[k], BF) for k in kinds),
             pltpu.SemaphoreType.DMA((n,)), pltpu.SemaphoreType.DMA((n,)),
             pltpu.SemaphoreType.DMA((n, 36)), pltpu.SemaphoreType.DMA((n, 36))],
-        compiler_params=pltpu.CompilerParams(collective_id=cid, has_side_effects=True, vmem_limit_bytes=60 << 20),
+        compiler_params=pltpu.CompilerParams(collective_id=cid, has_side_effects=True, vmem_limit_bytes=VMEM),
         name="gather",
     )(*blocks)
 
 PIECE = {"wide": (8, 2048), "tall": (64, 256)}
 SLOTS = 4
-
-
-def scatter_scratch(kinds):
-    n, out = len(kinds), {}
+VMEM = 67043328
+
+
+def scatter_scratch(kinds, far=""):
+    n, out, away = len(kinds), {}, {}
     for m, kind in enumerate(kinds):
         p = PIECE[kind]
         for phase, lead in ((1, (3, 2, 4, 4)), (2, (3, 2, 4)), (3, (3, 2))):
             for letter in "ABC":
-                out[f"{letter}{phase}", m] = pltpu.VMEM((*lead, *p), BF)
+                if phase == 1 and letter in far:
+                    away[f"{letter}1", m] = jax.ShapeDtypeStruct((*lead, *p), BF)
+                else:
+                    out[f"{letter}{phase}", m] = pltpu.VMEM((*lead, *p), BF)
             if phase > 1:
                 for letter in "AB":
                     out[f"{letter}s{phase}", m] = pltpu.VMEM((*lead, *p), BF)
@@ -134,15 +138,18 @@
     for kind in dict.fromkeys(kinds):
         out["slot", kind] = pltpu.VMEM((SLOTS, 4, 4, *PIECE[kind]), BF)
         out["slot_sem", kind] = pltpu.SemaphoreType.DMA((SLOTS,))
+        if far:
+            out["land", kind] = pltpu.VMEM((2, 2, 4, 4, *PIECE[kind]), BF)
+            out["land_sem", kind] = pltpu.SemaphoreType.DMA((2, 2))
     out["out_sem"] = pltpu.SemaphoreType.DMA((n,))
     out["send"] = pltpu.SemaphoreType.DMA((n, 54))
     out["recv"] = pltpu.SemaphoreType.DMA((n, 54))
-    return out
+    return out, away
 
 
 class Scatter:
-    def __init__(self, kinds, src, dst, has):
-        self.kinds, self.src, self.dst, self.has = kinds, src, dst, has
+    def __init__(self, kinds, src, dst, has, far=""):
+        self.kinds, self.src, self.dst, self.has, self.far = kinds, src, dst, has, far
         self.at, self.left, self.right = place()
         self.by = [[lax.rem(a + o, 4) for a in self.at] for o in range(4)]
         ms = range(len(kinds))
@@ -225,10 +232,26 @@
     def roles(self, h):
         return (("As", h, 2), ("Bs", 1 - h, self.ahead(1 - h)), ("Co", h, self.ahead(h)), ("Ko", h, 0))
 
+    def landed(self, m, c, h):
+        kind = self.kinds[m]
+        k = (c * 2 + h) % 2
+        return [pltpu.make_async_copy(self.has[f"{letter}1", m].at[c, d], self.has["land", kind].at[k, i], self.has["land_sem", kind].at[k, i])
+            for i, (letter, d) in enumerate((("C", h), ("B", 1 - h)))]
+
+    def fetch(self, m, c, h):
+        for letter, d, copy in zip("CB", (h, 1 - h), self.landed(m, c, h)):
+            self.copy(letter, 1, m, c, d).wait_recv()
+            copy.start()
+
     def total(self, phase, m, c, h):
-        self.copy("C", phase, m, c, h).wait_recv()
-        self.copy("B", phase, m, c, 1 - h).wait_recv()
-        one, two = self.has[f"C{phase}", m].at[c, h], self.has[f"B{phase}", m].at[c, 1 - h]
+        if phase == 1 and self.far:
+            for copy in self.landed(m, c, h):
+                copy.wait()
+            one, two = (self.has["land", self.kinds[m]].at[(c * 2 + h) % 2, i] for i in (0, 1))
+        else:
+            self.copy("C", phase, m, c, h).wait_recv()
+            self.copy("B", phase, m, c, 1 - h).wait_recv()
+            one, two = self.has[f"C{phase}", m].at[c, h], self.has[f"B{phase}", m].at[c, 1 - h]
         order = ORDERS[c]
         if phase == 1:
             own = self.take(m, 1, c, h)
@@ -259,16 +282,18 @@
     def out(self, m):
         return pltpu.make_async_copy(self.has["G", m], self.dst[m], self.has["out_sem"].at[m])
 
-    def steps(self):
-        ms = range(len(self.kinds))
+    def groups(self):
+        ms, flows = range(len(self.kinds)), [(c, d) for c in range(3) for d in (0, 1)]
+        out = []
         for phase in (1, 2, 3):
             for what in (self.combine, self.total):
                 for m in ms:
-                    for c in range(3):
-                        for d in (0, 1):
-                            yield functools.partial(what, phase, m, c, d)
-        for m in ms:
-            yield lambda m=m: self.out(m).start()
+                    group = [functools.partial(what, phase, m, *flow) for flow in flows]
+                    if phase == 1 and what == self.total and self.far:
+                        ahead = [functools.partial(self.fetch, m, *flow) for flow in flows]
+                        group = ahead[:2] + [step for i in range(6) for step in (group[i], *ahead[i + 2:i + 3])]
+                    out.append(group)
+        return out + [[lambda m=m: self.out(m).start() for m in ms]]
 
     def end(self):
         for m in range(len(self.kinds)):
@@ -288,27 +313,36 @@
     greet(it.left, it.right)
     for m in range(n):
         it.send(m)
-    for step in it.steps():
-        step()
+    for group in it.groups():
+        for step in group:
+            step()
     it.end()
 
 
 def scatter(kinds, whole, cid):
     n = len(kinds)
-    held = scatter_scratch(kinds)
+    held, _ = scatter_scratch(kinds)
     return pl.pallas_call(
         functools.partial(scatter_kernel, kinds, tuple(held)),
         out_shape=[jax.ShapeDtypeStruct(BLOCK[k], BF) for k in kinds],
         in_specs=[pl.BlockSpec(memory_space=pl.ANY)] * n,
         out_specs=[pl.BlockSpec(memory_space=pl.ANY)] * n,
         scratch_shapes=list(held.values()),
-        compiler_params=pltpu.CompilerParams(collective_id=cid, has_side_effects=True, vmem_limit_bytes=63 << 20),
+        compiler_params=pltpu.CompilerParams(collective_id=cid, has_side_effects=True, vmem_limit_bytes=VMEM),
         name="scatter",
     )(*(w.reshape(4, 4, 4, *BLOCK[k]) for w, k in zip(whole, kinds)))
 
 
-def matmul(a, w):
-    return jnp.dot(a, w, preferred_element_type=F32).astype(BF)
+def dot(a, b, over=(1, 0)):
+    return lax.dot_general(a, b, ((over[:1], over[1:]), ((), ())), preferred_element_type=F32)
+
+
+WIDTH = 512
+ROWS = 128
+PLAN1 = (2, 4, 5, 6, 7)
+PLAN0 = (2, 4, 6)
+ONCE = pl.Buffered(1)
+ANYWHERE = pl.BlockSpec(memory_space=pl.ANY)
 
 
 def normed(h):
@@ -317,11 +351,172 @@
     return (wide * scale).astype(BF)
 
 
-def layer(h, w):
-    a = normed(h)
-    gate = jnp.dot(a, w[0], preferred_element_type=F32)
-    up = jnp.dot(a, w[1], preferred_element_type=F32)
-    return h + matmul((jax.nn.silu(gate) * up).astype(BF), w[2])
+def normed_back(h, by_a, by_h):
+    wide, by_a = h.astype(F32), by_a.astype(F32)
+    scale = lax.rsqrt(jnp.mean(wide**2, -1, keepdims=True) + 1e-6)
+    along = jnp.mean(by_a * wide, -1, keepdims=True)
+    return (by_h.astype(F32) + (by_a * scale - wide * (along * scale**3)).astype(BF).astype(F32)).astype(BF)
+
+
+def specs(tokens, d, layer):
+    return (pl.BlockSpec((1, WIDTH, d), lambda i: (layer, i, 0)), pl.BlockSpec((1, d, WIDTH), lambda i: (layer, 0, i)),
+        pl.BlockSpec((tokens, WIDTH), lambda i: (0, i)), pl.BlockSpec((WIDTH, d), lambda i: (i, 0)), pl.BlockSpec((d, WIDTH), lambda i: (0, i)),
+        pl.BlockSpec((tokens, d), lambda i: (0, 0), pipeline_mode=ONCE))
+
+
+def rows_of(ref):
+    return [pl.ds(ROWS * r, ROWS) for r in range(ref.shape[0] // ROWS)]
+
+
+def first_kernel(h, w_gate, w_up, w_down, gate, up, out, a, acc):
+    tile = pl.program_id(0)
+
+    @pl.when(tile == 0)
+    def _():
+        acc[...] = jnp.zeros_like(acc)
+        for r in rows_of(h):
+            a[r] = normed(h[r])
+
+    g, u = dot(a[...], w_gate[0]), dot(a[...], w_up[0])
+    gate[...], up[...] = g, u
+    acc[...] += dot((jax.nn.silu(g) * u).astype(BF), w_down[0])
+
+    @pl.when(tile == pl.num_programs(0) - 1)
+    def _():
+        for r in rows_of(h):
+            out[r] = (h[r].astype(F32) + acc[r].astype(BF).astype(F32)).astype(BF)
+
+
+def last_kernel(h, by_y, w_gate, w_up, gate, up, by_down, a_t, a):
+    @pl.when(pl.program_id(0) == 0)
+    def _():
+        for r in rows_of(h):
+            a[r] = normed(h[r])
+            a_t[:, r] = a[r].T
+
+    g, u = dot(a[...], w_gate[0]), dot(a[...], w_up[0])
+    gate[...], up[...] = g, u
+    by_down[...] = dot((jax.nn.silu(g) * u).astype(BF), by_y[...], (0, 0)).astype(BF)
+
+
+def forward(h, by_y, weights, layer):
+    (tokens, d), hidden = h.shape, weights[0].shape[2]
+    w_down, w_in, across, by_w_down, _, states = specs(tokens, d, layer)
+    flat, wide = jax.ShapeDtypeStruct((tokens, d), BF), jax.ShapeDtypeStruct((tokens, hidden), F32)
+    call = functools.partial(pl.pallas_call, grid=(hidden // WIDTH,), compiler_params=pltpu.CompilerParams(vmem_limit_bytes=VMEM))
+    if by_y is None:
+        return call(first_kernel, in_specs=[states, w_in, w_in, w_down], out_specs=[across, across, states], out_shape=[wide, wide, flat],
+            scratch_shapes=[pltpu.VMEM((tokens, d), BF), pltpu.VMEM((tokens, d), F32)], name="first")(h, *weights)
+    turned = pl.BlockSpec((d, tokens), lambda i: (0, 0), pipeline_mode=ONCE)
+    return call(last_kernel, in_specs=[states, states, w_in, w_in], out_specs=[across, across, by_w_down, turned],
+        out_shape=[wide, wide, jax.ShapeDtypeStruct((hidden, d), BF), jax.ShapeDtypeStruct((d, tokens), BF)],
+        scratch_shapes=[pltpu.VMEM((tokens, d), BF)], name="last")(h, by_y, *weights[:2])
+
+
+def turn_back(refs, bufs, sems, by_h, a_t):
+    rows = rows_of(by_h)
+
+    def copies(r):
+        return [pltpu.make_async_copy(ref.at[rows[r]], buf.at[r % 2], sems.at[r % 2, i]) for i, (ref, buf) in enumerate(zip(refs, bufs))]
+
+    for copy in copies(0):
+        copy.start()
+    for r in range(len(rows)):
+        if r + 1 < len(rows):
+            for copy in copies(r + 1):
+                copy.start()
+        for copy in copies(r):
+            copy.wait()
+        h0, h1, by_y, by_a = (buf[r % 2] for buf in bufs)
+        a_t[:, rows[r]] = normed(h0).T
+        by_h[rows[r]] = normed_back(h1, by_a.astype(BF), by_y)
+
+
+def backward_kernel(kinds, plan, names, top, *refs):
+    refs = list(refs)
+    pop = lambda n: [refs.pop(0) for _ in range(n)]
+    n = len(kinds)
+    src = pop(n)
+    if top:
+        by_h, a_t, gate, up, w_down, w_gate, w_up = pop(7)
+    else:
+        given, (gate, up, w_down) = pop(4), pop(3)
+    dst, (by_gate_w, by_up_w, by_other) = pop(n), pop(3)
+    away = pop(2 * n)
+    if top:
+        acc, acc_sem = pop(2)
+    else:
+        (by_h, a_t), bufs, (sems,) = pop(2), pop(4), pop(1)
+    has = dict(zip(names, away + refs, strict=True))
+    it = Scatter(kinds, src, dst, has, "BC")
+    tile = pl.program_id(0)
+    groups = it.groups()
+
+    @pl.when(tile == 0)
+    def _():
+        it.begin()
+        greet(it.left, it.right)
+        for m in range(n):
+            it.send(m)
+        if top:
+            acc[...] = jnp.zeros_like(acc)
+        else:
+            turn_back(given, bufs, sems, by_h, a_t)
+
+    for number, group in zip(plan, groups):
+        @pl.when(tile == number)
+        def _():
+            for step in group:
+                step()
+
+    g, u = gate[...], up[...]
+    by_act = dot(by_h[...], w_down[0], (1, 1)).astype(BF).astype(F32)
+    part = jax.nn.sigmoid(g)
+    silu = g * part
+    by_up = (by_act * silu).astype(BF)
+    by_gate = (by_act * u * (part + silu * (1 - part))).astype(BF)
+    by_gate_w[...] = dot(a_t[...], by_gate).astype(BF)
+    by_up_w[...] = dot(a_t[...], by_up).astype(BF)
+    if top:
+        acc[...] += dot(by_gate, w_gate[0], (1, 1)) + dot(by_up, w_up[0], (1, 1))
+    else:
+        by_other[...] = dot((silu * u).astype(BF), by_h[...], (0, 0)).astype(BF)
+
+    @pl.when(tile == pl.num_programs(0) - 1)
+    def _():
+        if top:
+            pltpu.make_async_copy(acc, by_other, acc_sem).start()
+        for group in groups[len(plan):]:
+            for step in group:
+                step()
+        it.end()
+        if top:
+            pltpu.make_async_copy(acc, by_other, acc_sem).wait()
+
+
+def backward(kinds, plan, whole, layer, states, gate, up, weights, cid):
+    top, n = layer > 0, len(kinds)
+    held, away = scatter_scratch(kinds, "BC")
+    tokens, hidden = gate.shape
+    d = weights[0].shape[1]
+    w_down, w_in, across, by_w_down, by_w_in, flat = specs(tokens, d, layer)
+    turned = pl.BlockSpec((d, tokens), lambda i: (0, 0), pipeline_mode=ONCE)
+    args = [*(w.reshape(4, 4, 4, *BLOCK[k]) for w, k in zip(whole, kinds)), *states, gate, up, weights[2], *weights[:2 * top]]
+    ins = [*[ANYWHERE] * n, *([flat, turned] if top else [ANYWHERE] * 4), across, across, w_down, *[w_in] * (2 * top)]
+    outs = [*[ANYWHERE] * n, by_w_in, by_w_in, ANYWHERE if top else by_w_down, *[ANYWHERE] * len(away)]
+    shapes = [*(jax.ShapeDtypeStruct(BLOCK[k], BF) for k in kinds), *[jax.ShapeDtypeStruct((d, hidden), BF)] * 2,
+        jax.ShapeDtypeStruct((tokens, d), F32) if top else jax.ShapeDtypeStruct((hidden, d), BF), *away.values()]
+    if top:
+        scratch = [pltpu.VMEM((tokens, d), F32), pltpu.SemaphoreType.DMA]
+    else:
+        scratch = [pltpu.VMEM((tokens, d), BF), pltpu.VMEM((d, tokens), BF), *[pltpu.VMEM((2, ROWS, d), BF)] * 3, pltpu.VMEM((2, ROWS, d), F32),
+            pltpu.SemaphoreType.DMA((2, 4))]
+    return pl.pallas_call(
+        functools.partial(backward_kernel, kinds, plan, (*away, *held), top),
+        grid=(hidden // WIDTH,), in_specs=ins, out_specs=outs, out_shape=shapes, scratch_shapes=scratch + list(held.values()),
+        compiler_params=pltpu.CompilerParams(collective_id=cid, has_side_effects=True, vmem_limit_bytes=VMEM),
+        name="backward",
+    )(*args)[:n + 3]
 
 
 def adamw(w, m, v, g):
@@ -336,16 +531,13 @@
         weights, m, v = (arrays[i : i + 3] for i in (0, 3, 6))
         me = lax.axis_index("dp")
         layers = weights[0].shape[0]
-        h, backs = x[0], []
-        for number in range(layers):
-            h, back = jax.vjp(layer, h, tuple(w[number] for w in weights))
-            backs.append(back)
-        by_h, sums = dy[0], [None] * layers
-        for number in reversed(range(layers)):
-            by_h, by_w = backs[number](by_h)
-            sums[number] = by_w
-        for number in reversed(range(layers)):
-            sums[number] = scatter(KINDS, sums[number], 1)
+        assert layers == 2
+        h0, by_y = x[0], dy[0]
+        gate0, up0, h1 = forward(h0, None, weights, 0)
+        gate1, up1, by_down1, a_t = forward(h1, by_y, weights, 1)
+        down1, by_gate1, by_up1, by_a1 = backward(("tall",), PLAN1, [by_down1], 1, [by_y, a_t], gate1, up1, weights, 3)
+        top1, top2, *by0 = backward(("wide", "wide"), PLAN0, [by_gate1, by_up1], 0, [h0, h1, by_y, by_a1], gate0, up0, weights, 4)
+        sums = [scatter(KINDS, by0, 1), [top1, top2, down1]]
         new = []
         for i, kind in enumerate(KINDS):
             w = lax.dynamic_slice_in_dim(weights[i], me * BLOCK[kind][0], BLOCK[kind][0], axis=1)

time: 965 us -> 806 us (0.84)
  matrix products: 326 us -> 0 us
  Pallas kernels: 558 us -> 735 us
    dot_general x15 -> x0, matrix products: 326 us -> none  [the longest x5 114 us: layer(): up = jnp.dot(a, w[1], preferred_element_type=F32)]
    pallas_call x0 -> x4, Pallas kernels: none -> 324 us  [the longest x2 226 us: backward(): pl.pallas_call(functools.partial(backward_kernel, kinds, plan, (*away, *h...]
    pallas_call x2 -> x1, Pallas kernels: 290 us -> 142 us  [scatter(): pl.pallas_call(functools.partial(scatter_kernel, kinds, tuple(held)), out...]
where the time goes in v2:
time: 806 us; the launch traced here: 798 us
  Pallas kernels  735 us (91%)
  other arithmetic  59.7 us (7%)
    pallas_call x1, Pallas kernels, gather(): pl.pallas_call(functools.partial(gather_kernel, kinds), out_shape=[jax.Sh...  268 us
    pallas_call x2, Pallas kernels, backward(): pl.pallas_call(functools.partial(backward_kernel, kinds, plan, (*away, *h...  226 us
    pallas_call x1, Pallas kernels, scatter(): pl.pallas_call(functools.partial(scatter_kernel, kinds, tuple(held)), out...  142 us
    another operation x3, other arithmetic, step(): jnp.stack([whole[number * 3 + i].reshape(weights[i].shape[1:]) for number...  51.8 us
    pallas_call x1, Pallas kernels, forward(): call(first_kernel, in_specs=[states, w_in, w_in, w_down], out_specs=[acro...  49.8 us
    pallas_call x1, Pallas kernels, forward(): call(last_kernel, in_specs=[states, states, w_in, w_in], out_specs=[acros...  48.3 us

profile of v2, /device:TPU:0, one launch (start us, length us, event | category | flops | bytes accessed | tf_op | source)
XLA Modules:
  0.0 798.5 jit_solution(16716652401132276630)
XLA Ops:
  0.6 49.8 %first.1 = (f32[1024,4096]{1,0:T(8,128)}, f32[1024,4096]{1,0:T(8,128)}, bf16[1024,1536]{1,0:T(8,128)(2,1)}) custom-call(bf16[1024,1536]{1,0:T(8,128)(2,1)} %bitcast.35, bf16[2,1536,4096]{2,1,0:T(8,128)(2,1)} %refs_6_.1, bf16[2,1536,4096]{2,1,0:T(8,128)(2,1)} %refs_7_.1, bf16[2,4096,1536]{2,1,0:T(8,128)(2,1)} %refs_8_.1), custom_call_target="tpu_custom_call" | custom-call | tf_op jit(solution)/shard_map/first/pallas_call | solution.py:408
  50.5 48.3 %last.1 = (f32[1024,4096]{1,0:T(8,128)}, f32[1024,4096]{1,0:T(8,128)}, bf16[4096,1536]{1,0:T(8,128)(2,1)}, bf16[1536,1024]{1,0:T(8,128)(2,1)}) custom-call(bf16[1024,1536]{1,0:T(8,128)(2,1)} %get-tuple-element.34.h.refs_3_, bf16[1024,1536]{1,0:T(8,128)(2,1)} %bitcast.32, bf16[2,1536,4096]{2,1,0:T(8,128)(2,1)} %refs_6_.1, bf16[2,1536,4096]{2,1,0:T(8,128)(2,1)} %refs_7_.1), custom_call_target="tpu_custom_call" | custom-call | tf_op jit(solution)/shard_map/last/pallas_call | solution.py:411
  98.7 104.3 %backward.2 = (bf16[64,1536]{1,0:T(8,128)(2,1)}, bf16[1536,4096]{1,0:T(8,128)(2,1)}, bf16[1536,4096]{1,0:T(8,128)(2,1)}, f32[1024,1536]{1,0:T(8,128)}, bf16[3,2,...) custom-call(bf16[4,4,4,64,1536]{4,3,2,1,0:T(8,128)(2,1)} %bitcast.52, ...), custom_call_target="tpu_custom_call" | custom-call | tf_op jit(solution)/shard_map/backward/pallas_call | solution.py:514
  203.0 122.0 %backward.3 = (bf16[24,4096]{1,0:T(8,128)(2,1)}, bf16[24,4096]{1,0:T(8,128)(2,1)}, bf16[1536,4096]{1,0:T(8,128)(2,1)}, bf16[1536,4096]{1,0:T(8,128)(2,1)}, bf16[...) custom-call(bf16[4,4,4,24,4096]{4,3,2,1,0:T(8,128)(2,1)} %bitcast.37, ...), custom_call_target="tpu_custom_call" | custom-call | tf_op jit(solution)/shard_map/backward/pallas_call | solution.py:514
  325.0 142.4 %scatter.1 = (bf16[24,4096]{1,0:T(8,128)(2,1)}, bf16[24,4096]{1,0:T(8,128)(2,1)}, bf16[64,1536]{1,0:T(8,128)(2,1)}) custom-call(bf16[4,4,4,24,4096]{4,3,2,1,0:T(8,128)(2,1)} %bitcast.39, bf16[4,4,4,24,4096]{4,3,2,1,0:T(8,128)(2,1)} %bitcast.40, bf16[4,4,4,64,1536]{4,3,2,1,0:T(8,128)(2,1)} %bitcast.41), custom_call_target="tpu_custom_call" | custom-call | tf_op jit(solution)/shard_map/scatter/pallas_call | solution.py:325
  467.5 3.2 fusion.10
  470.7 0.8 slice_bitcast_fusion
  471.5 4.6 fusion.2
  476.1 0.8 slice_bitcast_fusion.1
  476.9 0.8 slice_bitcast_fusion.2
  477.6 268.5 %gather.1 = (bf16[4,4,4,24,4096]{4,3,2,1,0:T(8,128)(2,1)}, bf16[4,4,4,24,4096]{4,3,2,1,0:T(8,128)(2,1)}, bf16[4,4,4,64,1536]{4,3,2,1,0:T(8,128)(2,1)}, bf16[4,4,...) custom-call(bf16[24,4096]{1,0:T(8,128)(2,1)} %get-tuple-element.73.refs_0_, ...), custom_call_target="tpu_custom_call" | custom-call | tf_op jit(solution)/shard_map/gather/pallas_call | solution.py:105
  746.1 0.0 copy-start
  746.1 0.0 slice-start
  746.1 0.0 slice-start.1
  746.1 0.0 slice-start.3
  746.1 0.0 slice-start.4
  746.2 25.1 %pad_maximum_fusion.2 = bf16[2,4096,1536]{2,1,0:T(8,128)(2,1)} fusion(bf16[1,4096,1536]{2,1,0:T(8,128)(2,1)} %bitcast.51, bf16[1,4096,1536]{2,1,0:T(8,128)(2,1)} %bitcast.50), kind=kLoop, calls=%fused_computation.2 | loop fusion | flops 12582912 | bytes 50331648 | tf_op jit(solution)/shard_map/stack | solution.py:547
  771.3 0.0 copy-done
  771.3 16.9 %pad_maximum_fusion.1 = bf16[2,1536,4096]{2,1,0:T(8,128)(2,1)} fusion(bf16[1,1536,4096]{2,1,0:T(8,128)(2,1)} %bitcast.49, bf16[1,1536,4096]{2,1,0:T(8,128)(2,1)S(1)} %bitcast.48), kind=kLoop, calls=%fused_computation.1 | loop fusion | flops 12582912 | bytes 50331648 | tf_op jit(solution)/shard_map/stack | solution.py:547
  788.2 0.0 slice-done
  788.2 0.0 slice-done.1
  788.2 0.0 slice-done.3
  788.2 0.0 slice-done.4
  788.3 9.8 %pad_maximum_fusion = bf16[2,1536,4096]{2,1,0:T(8,128)(2,1)} fusion(bf16[1,1536,4096]{2,1,0:T(8,128)(2,1)S(1)} %bitcast.47, bf16[1,1536,4096]{2,1,0:T(8,128)(2,1)S(1)} %bitcast.44), kind=kLoop, calls=%fused_computation | loop fusion | flops 12582912 | bytes 50331648 | tf_op jit(solution)/shard_map/stack | solution.py:547
  (6 shorter events, 0.0 us)
Async XLA Ops:
  746.1 25.2 %copy-start = (bf16[4,4,4,24,4096]{4,3,2,1,0:T(8,128)(2,1)S(1)}, bf16[4,4,4,24,4096]{4,3,2,1,0:T(8,128)(2,1)}, u32[]{:S(2)}) copy-start(bf16[4,4,4,24,4096]{4,3,2,1,0:T(8,128)(2,1)} %get-tuple-element.55) | copy-start | bytes 37748740
  746.1 42.1 %slice-start = ((s8[12582912]{0:T(1024)(128)(4,1)}), s8[4194304]{0:T(1024)(128)(4,1)S(1)}, s32[]{:S(2)}) async-start(s8[12582912]{0:T(1024)(128)(4,1)} %bitcast.42), calls=%async_computation | async-start | bytes 8388608
  746.1 42.1 %slice-start.1 = ((s8[12582912]{0:T(1024)(128)(4,1)}), s8[4194304]{0:T(1024)(128)(4,1)S(1)}, s32[]{:S(2)}) async-start(s8[12582912]{0:T(1024)(128)(4,1)} %bitcast.42), calls=%async_computation.1 | async-start | bytes 8388608
  746.1 42.1 %slice-start.3 = ((s8[12582912]{0:T(1024)(128)(4,1)}), s8[4194304]{0:T(1024)(128)(4,1)S(1)}, s32[]{:S(2)}) async-start(s8[12582912]{0:T(1024)(128)(4,1)} %bitcast.45), calls=%async_computation.3 | async-start | bytes 8388608
  746.1 42.1 %slice-start.4 = ((s8[12582912]{0:T(1024)(128)(4,1)}), s8[4194304]{0:T(1024)(128)(4,1)S(1)}, s32[]{:S(2)}) async-start(s8[12582912]{0:T(1024)(128)(4,1)} %bitcast.45), calls=%async_computation.4 | async-start | bytes 8388608
  771.3 17.0 %slice-start.2 = ((s8[12582912]{0:T(1024)(128)(4,1)}), s8[4194304]{0:T(1024)(128)(4,1)S(1)}, s32[]{:S(2)}) async-start(s8[12582912]{0:T(1024)(128)(4,1)} %bitcast.42), calls=%async_computation.2 | async-start | bytes 8388608
  771.3 17.0 %slice-start.5 = ((s8[12582912]{0:T(1024)(128)(4,1)}), s8[4194304]{0:T(1024)(128)(4,1)S(1)}, s32[]{:S(2)}) async-start(s8[12582912]{0:T(1024)(128)(4,1)} %bitcast.45), calls=%async_computation.5 | async-start | bytes 8388608

commit v3 on v0

v3 whole, which is shorter than its diff:
```python
import functools
import jax, jax.numpy as jnp
from jax import lax
from jax.experimental import pallas as pl
from jax.experimental.pallas import tpu as pltpu
MESH = pl.DeviceIdType.MESH
BF, F32 = jnp.bfloat16, jnp.float32
ORDERS = ((0, 1, 2), (1, 2, 0), (2, 0, 1))
STRIDE = (16, 4, 1)

from jax.sharding import PartitionSpec as P

NAMES = ("w_gate", "w_up", "w_down")
KINDS = ("wide", "wide", "tall")


def place():
    me = lax.axis_index("dp")
    at = (me // 16, (me // 4) % 4, me % 4)
    def step(axis, by):
        return me + (lax.rem(at[axis] + by, 4) - at[axis]) * STRIDE[axis]
    right = [step(a, 1) for a in range(3)]
    left = [step(a, 3) for a in range(3)]
    return at, left, right

def greet(left, right):
    barrier = pltpu.get_barrier_semaphore()
    for to in (*left, *right):
        pl.semaphore_signal(barrier, inc=1, device_id={"dp": to}, device_id_type=MESH)
    pl.semaphore_wait(barrier, 6)

def piece(kind, color, half):
    if kind == "wide":
        return (color, slice(None), slice(None) if half is None else pl.ds(2048 * half, 2048))
    return (slice(None), slice(None), pl.ds(512 * color, 512) if half is None else pl.ds(512 * color + 256 * half, 256))

BLOCK = {"wide": (3, 8, 4096), "tall": (8, 8, 1536)}
PIECE = (8, 2048)


def over(n):
    def run(body):
        lax.fori_loop(0, n, lambda i, _: body(i), None)

    return run


WIDE = BLOCK["wide"]
VMEM = 67043328


def sums_scratch(n):
    near, away = {}, {}
    for m in range(n):
        for phase, lead in ((1, (3, 2, 4, 4)), (2, (3, 2, 4)), (3, (3, 2))):
            for letter in "ABC":
                if phase == 1:
                    away[f"{letter}1", m] = jax.ShapeDtypeStruct((*lead, *PIECE), BF)
                else:
                    near[f"{letter}{phase}", m] = pltpu.VMEM((*lead, *PIECE), BF)
    near["pass1"] = pltpu.VMEM((3, 2, 4, 4, *PIECE), BF)
    for phase, lead in ((2, (3, 2, 4)), (3, (3, 2))):
        near[f"send{phase}"] = pltpu.VMEM((2, *lead, *PIECE), BF)
        near[f"keep{phase}"] = pltpu.VMEM((2, *lead, *PIECE), F32)
    near["G"] = pltpu.VMEM((n, 3, 2, *PIECE), BF)
    near["land"] = pltpu.VMEM((2, 3, 2, 4, 4, *PIECE), BF)
    dma = pltpu.SemaphoreType.DMA
    near |= {"land_sem": dma((2,)), "sent": dma((n, 9)), "came1": dma((n, 3, 3)), "came": dma((n, 6))}
    return near, away


class Sums:
    def __init__(self, src, has):
        self.src, self.has = src, has
        self.at, self.left, self.right = place()
        self.by = [[lax.rem(a + o, 4) for a in self.at] for o in range(4)]

    def own(self, m, c, o, half):
        idx = [slice(None)] * 3
        idx[ORDERS[c][0]] = self.by[o][ORDERS[c][0]]
        return self.src[m].at[(*idx, *piece("wide", c, half))]

    def copy(self, letter, phase, m, c, d):
        k = "ABC".index(letter)
        to = self.has[f"{letter}{phase}", m]
        if c is None:
            src = dst = to
        elif d is None:
            src = dst = to.at[c]
        else:
            dst = to.at[c, d]
            if letter == "C":
                src = self.has["pass1"].at[c, d] if phase == 1 else self.has[f"A{phase}", m].at[c, d]
            elif phase > 1:
                src = self.has[f"send{phase}"].at[k, c, d]
            else:
                src = self.own(m, c, *((2, d) if letter == "A" else (1 + 2 * d, 1 - d)))
        came = self.has["came1"].at[m, k, c or 0] if phase == 1 else self.has["came"].at[m, phase * 3 - 6 + k]
        return pltpu.make_async_remote_copy(src_ref=src, dst_ref=dst, send_sem=self.has["sent"].at[m, phase * 3 - 3 + k], recv_sem=came,
            device_id={"dp": (self.left if d else self.right)[ORDERS[c or 0][phase - 1]]}, device_id_type=MESH)

    def send(self, letter, m, phase=1, colors=(0, 1, 2)):
        for c in colors:
            for d in (0, 1):
                self.copy(letter, phase, m, c, d).start()

    def came(self, letters, phase, m):
        for letter in letters:
            self.copy(letter, phase, m, None, None).wait_recv()

    def sent(self, letters, phase, m):
        for letter in letters:
            self.copy(letter, phase, m, None, None).wait_send()

    def fetch(self, what, m, c, slot):
        land, sem = self.has["land"].at[slot], self.has["land_sem"].at[slot]
        for i, letter in ((0, "A"),) if what == "c" else ((0, "C"), (2, "B")):
            self.copy(letter, 1, m, c, None).wait_recv()
            pltpu.make_async_copy(self.has[f"{letter}1", m].at[c], land.at[i], sem).start()
        for d in (0, 1):
            pltpu.make_async_copy(self.own(m, c, 1 + 2 * d if what == "c" else 0, d), land.at[1, d], sem).start()

    def first(self, what, m, c, slot):
        land = self.has["land"].at[slot]
        got = land.at[0:2] if what == "c" else land
        pltpu.make_async_copy(got, got, self.has["land_sem"].at[slot]).wait()
        if what == "c":
            if m > 0 and c == 0:
                self.sent("C", 1, m - 1)
            to = self.has["pass1"]

            @over(2)
            def _(d):
                @over(4)
                def _(i):
                    @over(4)
                    def _(j):
                        to[c, d, i, j] = (land[0, d, i, j].astype(F32) + land[1, d, i, j].astype(F32)).astype(BF)

            self.send("C", m, 1, (c,))
            return
        if m > 0 and c == 0:
            self.sent("AB", 2, m - 1)
        axis = ORDERS[c][1]

        def whole(h, t, i):
            at = (t, i) if axis < ORDERS[c][2] else (i, t)
            return land[(1, h, *at)].astype(F32) + land[(0, h, *at)].astype(F32) + land[(2, 1 - h, *at)].astype(F32)

        @over(2)
        def _(h):
            @over(2)
            def _(k):
                d, t, u = self.role(axis, h, k)

                @over(4)
                def _(i):
                    self.has["send2"][k, c, d, i] = whole(h, t, i).astype(BF)
                    self.has["keep2"][k, c, h, i] = whole(h, u, i)

        self.send("A", m, 2, (c,))
        self.send("B", m, 2, (c,))

    def role(self, axis, h, k):
        turn = k * (1 - 2 * h)
        return h + turn, lax.rem(self.at[axis] + 2 + turn, 4), lax.rem(self.at[axis] + k * (1 + 2 * h), 4)

    def later(self, what, phase, m):
        a, b, c_ = (self.has[f"{letter}{phase}", m] for letter in "ABC")
        keep = self.has[f"keep{phase}"]
        if what == "c":
            self.came("A", phase, m)

            @over(3)
            def _(c):
                @over(2)
                def _(d):
                    if phase == 3:
                        a[c, d] = (a[c, d].astype(F32) + keep[1, c, d]).astype(BF)
                    else:
                        @over(4)
                        def _(i):
                            a[c, d, i] = (a[c, d, i].astype(F32) + keep[1, c, d, i]).astype(BF)

            self.send("C", m, phase)
            return
        self.came("CB", phase, m)
        if phase == 3:
            @over(3)
            def _(c):
                @over(2)
                def _(h):
                    self.has["G"][m, c, h] = (keep[0, c, h] + c_[c, h].astype(F32) + b[c, 1 - h].astype(F32)).astype(BF)

            return
        if m > 0:
            self.sent("AB", 3, m - 1)
        for c in range(3):
            def whole(h, t):
                return keep[0, c, h, t] + c_[c, h, t].astype(F32) + b[c, 1 - h, t].astype(F32)

            @over(2)
            def _(h):
                @over(2)
                def _(k):
                    d, t, u = self.role(ORDERS[c][2], h, k)
                    self.has["send3"][k, c, d] = whole(h, t).astype(BF)
                    self.has["keep3"][k, c, h] = whole(h, u)

        self.send("A", m, 3)
        self.send("B", m, 3)

    def end(self, first, last):
        for m in range(first, last + 1):
            self.sent("AB" + "C" * (m == last), 1, m)
            for phase in (2, 3):
                self.sent("C" + "AB" * (m == last), phase, m)


ORDER = ((1, 2), (1, 0), (1, 1), (0, 2), (0, 0), (0, 1))
KIND_OF = tuple(KINDS[i] for _, i in ORDER)
SLOT_OF = tuple(KIND_OF[:m].count(k) for m, k in enumerate(KIND_OF))


def gather_scratch():
    out = {}
    for kind in dict.fromkeys(KIND_OF):
        n = KIND_OF.count(kind)
        out["moments", kind] = pltpu.VMEM((n, 2, *BLOCK[kind]), F32)
        out["w", kind] = pltpu.VMEM((n, *BLOCK[kind]), BF)
    return out


class Gather:
    def __init__(self, it, weights, moments, whole, new, has, sems):
        self.it, self.weights, self.moments, self.whole, self.new, self.has = it, weights, moments, whole, new, has
        self.load_sem, self.save_sem, self.mine_sem, self.ssem, self.rsem = sems

    def held(self, m):
        return self.has["w", KIND_OF[m]].at[SLOT_OF[m]]

    def loads(self, m):
        layer, i = ORDER[m]
        me = lax.axis_index("dp")
        refs = [self.weights[i].at[layer, me], *(ref.at[layer] for ref in self.moments[i])]
        bufs = [self.held(m), *(self.has["moments", KIND_OF[m]].at[SLOT_OF[m], j] for j in (0, 1))]
        return [pltpu.make_async_copy(ref, buf, self.load_sem.at[m, j]) for j, (ref, buf) in enumerate(zip(refs, bufs))]

    def saves(self, m):
        layer, i = ORDER[m]
        return [pltpu.make_async_copy(self.has["moments", KIND_OF[m]].at[SLOT_OF[m], j], self.new[i][j].at[layer], self.save_sem.at[m, j])
            for j in (0, 1)]

    def mine(self, m):
        at = self.it.at
        return pltpu.make_async_copy(self.held(m), self.whole[m].at[at[0], at[1], at[2]], self.mine_sem.at[m])

    def adamw(self, m):
        for copy in self.loads(m):
            copy.wait()
        w, moments, g = self.held(m), self.has["moments", KIND_OF[m]].at[SLOT_OF[m]], self.it.has["G"].at[m]

        @over(3)
        def _(c):
            @over(2)
            def _(h):
                @over(4)
                def _(i):
                    from_g = (c, h, slice(None), pl.ds(pl.multiple_of(512 * i, 512), 512))
                    if KIND_OF[m] == "wide":
                        at = (c, slice(None), pl.ds(pl.multiple_of(2048 * h + 512 * i, 512), 512))
                    else:
                        at = (4 * h + i, slice(None), pl.ds(pl.multiple_of(512 * c, 512), 512))
                    w[at], moments[(0, *at)], moments[(1, *at)] = adamw(w[at].astype(F32), moments[(0, *at)], moments[(1, *at)], g[from_g].astype(F32))

        self.mine(m).start()
        for copy in self.saves(m):
            copy.start()

    def msg(self, m, color, phase, d, fwd):
        order, at = ORDERS[color], self.it.at
        axis = order[phase]
        idx = list(at)
        if fwd:
            idx[axis] = self.it.by[3 if d == 0 else 1][axis]
        for p in range(phase + 1, 3):
            idx[order[p]] = slice(None)
        part = piece(KIND_OF[m], color, d if fwd else None)
        dst = self.whole[m].at[(*idx, *part)]
        src = self.held(m).at[part] if phase == 2 and not fwd else dst
        return self.sets(m, phase, fwd, src, dst, (self.it.right if d == 0 else self.it.left)[axis])

    def sets(self, m, phase, fwd, src, dst, to):
        k = phase * 2 + int(fwd)
        return pltpu.make_async_remote_copy(src_ref=src, dst_ref=dst, send_sem=self.ssem.at[m, k], recv_sem=self.rsem.at[m, k],
            device_id={"dp": to}, device_id_type=MESH)

    def all(self, m, phase, fwd):
        much = self.whole[m].at[(*(0,) * phase, slice(0, 1 if fwd else 2))]
        return self.sets(m, phase, fwd, much, much, self.it.right[0])

    def send(self, m, phase, fwd):
        if fwd:
            self.all(m, phase, False).wait_recv()
        elif phase < 2:
            self.all(m, phase + 1, True).wait_recv()
        if not fwd and phase == 1:
            self.mine(m).wait()
        for color in range(3):
            for d in (0, 1):
                self.msg(m, color, phase, d, fwd).start()

    def end(self):
        for m in range(len(ORDER)):
            for copy in self.saves(m):
                copy.wait()
            self.all(m, 0, True).wait_recv()
            for phase in range(3):
                for fwd in (False, True):
                    self.all(m, phase, fwd).wait_send()


def dot(a, b, over=(1, 0)):
    return lax.dot_general(a, b, ((over[:1], over[1:]), ((), ())), preferred_element_type=F32)


WIDTH = 512
ROWS = 128
ONCE = pl.Buffered(1)
ANYWHERE = pl.BlockSpec(memory_space=pl.ANY)


def normed(h):
    wide = h.astype(F32)
    scale = lax.rsqrt(jnp.mean(wide**2, -1, keepdims=True) + 1e-6)
    return (wide * scale).astype(BF)


def normed_back(h, by_a, by_h):
    wide, by_a = h.astype(F32), by_a.astype(F32)
    scale = lax.rsqrt(jnp.mean(wide**2, -1, keepdims=True) + 1e-6)
    along = jnp.mean(by_a * wide, -1, keepdims=True)
    return (by_h.astype(F32) + (by_a * scale - wide * (along * scale**3)).astype(BF).astype(F32)).astype(BF)


PACKED = pl.BlockSpec((WIDTH // 64, *WIDE), lambda i: (i, 0, 0, 0))


def specs(tokens, d, layer):
    return (pl.BlockSpec((1, WIDTH, d), lambda i: (layer, i, 0)), pl.BlockSpec((1, d, WIDTH), lambda i: (layer, 0, i)),
        pl.BlockSpec((tokens, WIDTH), lambda i: (0, i)), pl.BlockSpec((tokens, d), lambda i: (0, 0), pipeline_mode=ONCE))


def pack(out, tile):
    tile = tile.reshape(*out.shape[:-3], 8, 8, 1536)
    for c in range(3):
        for g in range(8):
            out[..., c, :, 512 * g:512 * g + 512] = tile[..., g, :, 512 * c:512 * c + 512].astype(BF)


def rows_of(ref):
    return [pl.ds(ROWS * r, ROWS) for r in range(ref.shape[0] // ROWS)]


def first_kernel(h, w_gate, w_up, w_down, gate, up, act, out, a, acc):
    tile = pl.program_id(0)

    @pl.when(tile == 0)
    def _():
        acc[...] = jnp.zeros_like(acc)
        for r in rows_of(h):
            a[r] = normed(h[r])

    g, u = dot(a[...], w_gate[0]), dot(a[...], w_up[0])
    gate[...], up[...] = g, u
    act[...] = (jax.nn.silu(g) * u).astype(BF)
    acc[...] += dot(act[...], w_down[0])

    @pl.when(tile == pl.num_programs(0) - 1)
    def _():
        for r in rows_of(h):
            out[r] = (h[r].astype(F32) + acc[r].astype(BF).astype(F32)).astype(BF)


def last_kernel(h, by_y, w_gate, w_up, gate, up, by_down, a_t, a):
    @pl.when(pl.program_id(0) == 0)
    def _():
        for r in rows_of(h):
            a[r] = normed(h[r])
            a_t[:, r] = a[r].T

    g, u = dot(a[...], w_gate[0]), dot(a[...], w_up[0])
    gate[...], up[...] = g, u
    pack(by_down, dot((jax.nn.silu(g) * u).astype(BF), by_y[...], (0, 0)))


def forward(h, by_y, weights, layer):
    (tokens, d), hidden = h.shape, weights[0].shape[2]
    w_down, w_in, across, states = specs(tokens, d, layer)
    flat, wide = jax.ShapeDtypeStruct((tokens, d), BF), jax.ShapeDtypeStruct((tokens, hidden), F32)
    call = functools.partial(pl.pallas_call, grid=(hidden // WIDTH,), compiler_params=pltpu.CompilerParams(vmem_limit_bytes=VMEM))
    if by_y is None:
        return call(first_kernel, in_specs=[states, w_in, w_in, w_down], out_specs=[across, across, across, states], out_shape=[wide, wide, jax.ShapeDtypeStruct(wide.shape, BF), flat],
            scratch_shapes=[pltpu.VMEM((tokens, d), BF), pltpu.VMEM((tokens, d), F32)], name="first")(h, *weights)
    turned = pl.BlockSpec((d, tokens), lambda i: (0, 0), pipeline_mode=ONCE)
    return call(last_kernel, in_specs=[states, states, w_in, w_in], out_specs=[across, across, PACKED, turned],
        out_shape=[wide, wide, jax.ShapeDtypeStruct((64, *WIDE), BF), jax.ShapeDtypeStruct((d, tokens), BF)],
        scratch_shapes=[pltpu.VMEM((tokens, d), BF)], name="last")(h, by_y, *weights[:2])


def adamw(w, m, v, g):
    m = 0.9 * m + 0.1 * g
    v = 0.95 * v + 0.05 * g * g
    step = m * lax.rsqrt(v + 1e-8) + 0.1 * w
    return (w - 0.02 * step).astype(BF), m, v


PLAN = {
    "start": {
        (0, 0): (('A', 0),),
    },
    "top": {
        (1, 0): (('B', 0),),
        (3, 1): (('F', 'c', 0, 0, 0), ('F', 'c', 0, 1, 1),),
        (4, 0): (('P', 'c', 0, 0, 0), ('F', 'c', 0, 2, 0),),
        (4, 1): (('P', 'c', 0, 1, 1),),
        (5, 0): (('P', 'c', 0, 2, 0),),
    },
    "up": {
        (0, 0): (('F', 't', 0, 0, 1), ('F', 't', 0, 1, 0), ('A', 1),),
        (1, 0): (('P', 't', 0, 0, 1), ('F', 't', 0, 2, 1), ('B', 1),),
        (2, 0): (('P', 't', 0, 1, 0),),
        (3, 0): (('P', 't', 0, 2, 1),),
        (6, 0): (('F', 'c', 1, 0, 0), ('F', 'c', 1, 1, 1),),
        (7, 0): (('P', 'c', 1, 0, 0), ('F', 'c', 1, 2, 0),),
    },
    "mid": {
        (0, 0): (('P', 'c', 1, 1, 1), ('A', 2),),
        (1, 0): (('P', 'c', 1, 2, 0), ('O', 'c', 2, 0),),
        (5, 0): (('F', 't', 1, 0, 1), ('F', 't', 1, 1, 0), ('B', 2),),
    },
    "turn": {
        (0, 0): (('O', 't', 2, 0),),
        (1, 0): (('P', 't', 1, 0, 1), ('F', 't', 1, 2, 1),),
        (2, 0): (('P', 't', 1, 1, 0), ('F', 'c', 2, 0, 0),),
        (3, 0): (('P', 't', 1, 2, 1), ('F', 'c', 2, 1, 1),),
    },
    "down": {
        (0, 0): (('O', 'c', 3, 0), ('P', 'c', 2, 0, 0), ('F', 'c', 2, 2, 0),),
        (1, 0): (('O', 'c', 2, 1), ('P', 'c', 2, 1, 1),),
        (2, 0): (('O', 't', 3, 0), ('P', 'c', 2, 2, 0),),
        (6, 0): (('F', 't', 2, 0, 1),),
    },
    "low": {
        (0, 0): (('O', 't', 2, 1), ('F', 't', 2, 1, 0), ('A', 3),),
        (0, 1): (('P', 't', 2, 0, 1), ('F', 't', 2, 2, 1), ('B', 3),),
        (1, 0): (('O', 'c', 3, 1), ('P', 't', 2, 1, 0),),
        (1, 1): (('P', 't', 2, 2, 1),),
        (3, 0): (('F', 'c', 3, 0, 0), ('F', 'c', 3, 1, 1),),
        (3, 1): (('P', 'c', 3, 0, 0), ('F', 'c', 3, 2, 0),),
        (4, 0): (('P', 'c', 3, 1, 1),),
        (4, 1): (('P', 'c', 3, 2, 0),),
        (5, 1): (('O', 'c', 2, 2),),
        (6, 1): (('O', 't', 3, 1),),
    },
    "last": {
        (0, 0): (('F', 't', 3, 0, 1), ('F', 't', 3, 1, 0), ('A', 4),),
        (1, 0): (('O', 't', 2, 2),),
        (2, 0): (('P', 't', 3, 0, 1), ('F', 't', 3, 2, 1), ('B', 4),),
        (3, 0): (('P', 't', 3, 1, 0),),
        (4, 0): (('P', 't', 3, 2, 1),),
        (6, 0): (('O', 'c', 3, 2), ('F', 'c', 4, 0, 0), ('F', 'c', 4, 1, 1),),
        (7, 0): (('P', 'c', 4, 0, 0), ('F', 'c', 4, 2, 0),),
    },
}
TAIL = (
    ('P', 'c', 4, 1, 1), ('P', 'c', 4, 2, 0), ('u', 0), ('u', 1), ('g', 0, 2, 'o'), ('O', 'c', 2, 3),
    ('g', 1, 2, 'o'), ('O', 't', 3, 2), ('u', 2), ('g', 2, 2, 'o'), ('A', 5), ('F', 't', 4, 0, 1),
    ('F', 't', 4, 1, 0), ('g', 0, 2, 'f'), ('O', 't', 2, 3), ('P', 't', 4, 0, 1), ('P', 't', 4, 1, 0), ('F', 't', 4, 2, 1),
    ('g', 1, 2, 'f'), ('g', 2, 2, 'f'), ('P', 't', 4, 2, 1), ('B', 5), ('F', 'c', 5, 0, 0), ('F', 'c', 5, 1, 1),
    ('O', 'c', 3, 3), ('P', 'c', 5, 0, 0), ('P', 'c', 5, 1, 1), ('F', 'c', 5, 2, 0), ('g', 0, 1, 'o'), ('P', 'c', 5, 2, 0),
    ('O', 'c', 2, 4), ('g', 1, 1, 'o'), ('g', 2, 1, 'o'), ('O', 't', 3, 3), ('u', 3), ('g', 3, 2, 'o'),
    ('F', 't', 5, 0, 1), ('F', 't', 5, 1, 0), ('g', 0, 1, 'f'), ('O', 't', 2, 4), ('P', 't', 5, 0, 1), ('P', 't', 5, 1, 0),
    ('F', 't', 5, 2, 1), ('P', 't', 5, 2, 1), ('g', 1, 1, 'f'), ('g', 2, 1, 'f'), ('g', 3, 2, 'f'), ('O', 'c', 3, 4),
    ('O', 'c', 2, 5), ('g', 0, 0, 'o'), ('O', 't', 3, 4), ('u', 4), ('g', 4, 2, 'o'), ('g', 3, 1, 'o'),
    ('O', 't', 2, 5), ('g', 1, 0, 'o'), ('g', 4, 2, 'f'), ('O', 'c', 3, 5), ('g', 3, 1, 'f'), ('g', 0, 0, 'f'),
    ('O', 't', 3, 5), ('u', 5), ('g', 5, 2, 'o'), ('g', 4, 1, 'o'), ('g', 1, 0, 'f'), ('g', 5, 2, 'f'),
    ('g', 4, 1, 'f'), ('g', 2, 0, 'o'), ('g', 5, 1, 'o'), ('g', 3, 0, 'o'), ('g', 5, 1, 'f'), ('g', 2, 0, 'f'),
    ('g', 3, 0, 'f'), ('g', 4, 0, 'o'), ('g', 5, 0, 'o'), ('g', 4, 0, 'f'), ('g', 5, 0, 'f'),
)


def backward_kernel(names, by_down1, h0, h1, by_y, a_t, gate1, up1, act0, gate0, up0, *refs):
    refs = list(refs)
    pop = lambda n: [refs.pop(0) for _ in range(n)]
    weights, blocks, moments, whole, new = pop(3), pop(3), [pop(2) for _ in range(3)], pop(6), [pop(2) for _ in range(3)]
    by_gate1, by_up1, by_gate0, by_up0, by_down0, hid_gate, hid_up = pop(7)
    away = pop(18)
    states, turned, start_sem = pop(3)
    sems = pop(5)
    has = dict(zip(names, away + refs, strict=True))
    w_gate, w_up, w_down = weights
    it = Sums([by_down1, by_gate1, by_up1, by_down0, by_gate0, by_up0], has)
    (tokens, d), hidden = h0.shape, gate0.shape[1]
    tall, wide = pl.BlockSpec((WIDTH, d), lambda i: (i, 0)), pl.BlockSpec((d, WIDTH), lambda i: (0, i))
    across = pl.BlockSpec((tokens, WIDTH), lambda i: (0, i))
    cut = pl.BlockSpec((4, 4, 4, 3, 8, WIDTH), lambda i: (0, 0, 0, 0, 0, i))
    packed = pl.BlockSpec((1, 2, 4, *WIDE), lambda i: (i // 2, lax.rem(i, 2), 0, 0, 0, 0))

    def do(op):
        if op[0] in "AB":
            it.send(*op)
        elif op[0] == "F":
            it.fetch(*op[1:])
        elif op[0] == "P":
            it.first(*op[1:])
        else:
            it.later(*op[1:])

    def loop(stage, body, ins, outs, *at):
        def hook(sub):
            for (tile, where), ops in PLAN[stage].items():
                if where == sub:
                    @pl.when(pl.program_id(0) == tile)
                    def _():
                        for op in ops:
                            do(op)

        pltpu.emit_pipeline(functools.partial(body, hook), grid=(hidden // WIDTH,), in_specs=ins, out_specs=outs)(*at)

    def into(hook, gate, up, w_down, by_gate_w, hid_up, *hid_gate):
        hook(0)
        g, u = gate[...], up[...]
        by_act = dot(states[...], w_down[...], (1, 1)).astype(BF).astype(F32)
        part = jax.nn.sigmoid(g)
        silu = g * part
        hid_up[...] = (by_act * silu).astype(BF)
        by_gate = (by_act * u * (part + silu * (1 - part))).astype(BF)
        if hid_gate:
            hid_gate[0][...] = by_gate
        by_gate_w[...] = dot(turned[...], by_gate).reshape(by_gate_w.shape).astype(BF)
        hook(1)

    def of_up(hook, by_up, by_up_w):
        hook(0)
        by_up_w[...] = dot(turned[...], by_up[...]).reshape(by_up_w.shape).astype(BF)

    def down(hook, act, by_w):
        hook(0)
        pack(by_w, dot(act[...], states[...], (0, 0)))

    def back_to_states(acc, late0, late1, late_sem):
        acc[...] = jnp.zeros_like(acc)

        def more(hook, by_gate, by_up, w_gate, w_up):
            hook(0)
            acc[...] += dot(by_gate[...], w_gate[...], (1, 1)) + dot(by_up[...], w_up[...], (1, 1))

        loop("mid", more, [across, across, wide, wide], [], hid_gate, hid_up, w_gate.at[1], w_up.at[1])
        def copies(r):
            rows, slot = pl.ds(pl.multiple_of(128 * r, 128), 128), lax.rem(r, 2)
            return [pltpu.make_async_copy(ref.at[rows], buf.at[slot], late_sem.at[slot, i]) for i, (ref, buf) in enumerate(((h0, late0), (h1, late1)))]

        for copy in copies(0):
            copy.start()

        @over(tokens // 128)
        def _(r):
            for (tile, _), ops in PLAN["turn"].items():
                @pl.when(r == 2 * tile)
                def _():
                    for op in ops:
                        do(op)

            @pl.when(r + 1 < tokens // 128)
            def _():
                for copy in copies(r + 1):
                    copy.start()

            for copy in copies(r):
                copy.wait()
            rows, slot = pl.ds(pl.multiple_of(128 * r, 128), 128), lax.rem(r, 2)
            turned[:, rows] = normed(late0[slot]).T
            states[rows] = normed_back(late1[slot], acc[rows].astype(BF), states[rows])

    def tail(*bufs):
        last = Gather(it, blocks, moments, whole, new, dict(zip(gather_scratch(), bufs, strict=True)), sems)
        for m in range(len(ORDER)):
            for copy in last.loads(m):
                copy.start()
        for op in TAIL:
            if op[0] == "u":
                last.adamw(op[1])
            elif op[0] == "g":
                last.send(op[1], op[2], op[3] == "f")
            else:
                do(op)
        it.end(0, 5)
        last.end()

    early = [pltpu.make_async_copy(by_y, states, start_sem.at[0]), pltpu.make_async_copy(a_t, turned, start_sem.at[1])]
    for copy in early:
        copy.start()
    greet(it.left, it.right)
    for op in PLAN["start"][0, 0]:
        do(op)
    for copy in early:
        copy.wait()
    loop("top", into, [across, across, tall], [cut, across, across], gate1, up1, w_down.at[1], by_gate1, hid_up, hid_gate)
    loop("up", of_up, [across], [cut], hid_up, by_up1)
    pl.run_scoped(back_to_states, pltpu.VMEM((tokens, d), F32), *[pltpu.VMEM((2, 128, d), BF)] * 2, pltpu.SemaphoreType.DMA((2, 2)))
    loop("down", down, [across], [packed], act0, by_down0)
    loop("low", into, [across, across, tall], [cut, across], gate0, up0, w_down.at[0], by_gate0, hid_up)
    loop("last", of_up, [across], [cut], hid_up, by_up0)
    pl.run_scoped(tail, *gather_scratch().values())


def backward(by_down1, states, hidden_states, weights, moments, cid):
    near, away = sums_scratch(6)
    tokens, d = states[0].shape
    hidden = weights[0].shape[2]
    args = [by_down1.reshape(4, 4, 4, *WIDE), *states, *hidden_states, *weights, *(w.reshape(2, 64, *BLOCK[k]) for w, k in zip(weights, KINDS)), *(t.reshape(2, *BLOCK[k]) for pair, k in zip(moments, KINDS) for t in pair)]
    across = jax.ShapeDtypeStruct((tokens, hidden), BF)
    outs = [*(jax.ShapeDtypeStruct((4, 4, 4, *BLOCK[k]), BF) for k in KIND_OF), *(jax.ShapeDtypeStruct((2, *BLOCK[k]), F32) for k in KINDS for _ in range(2)),
        *[jax.ShapeDtypeStruct((4, 4, 4, *WIDE), BF)] * 5, across, across, *away.values()]
    dma = pltpu.SemaphoreType.DMA
    scratch = [pltpu.VMEM((tokens, d), BF), pltpu.VMEM((d, tokens), BF), dma((2,)),
        dma((6, 3)), dma((6, 2)), dma((6,)), dma((6, 6)), dma((6, 6))]
    out = pl.pallas_call(
        functools.partial(backward_kernel, (*away, *near)),
        in_specs=[ANYWHERE] * len(args), out_specs=[ANYWHERE] * len(outs), out_shape=outs, scratch_shapes=scratch + list(near.values()),
        compiler_params=pltpu.CompilerParams(collective_id=cid, has_side_effects=True, vmem_limit_bytes=VMEM),
        name="backward",
    )(*args)
    return out[:6], [[t.reshape(pair[0].shape) for t in out[6 + 2 * i:8 + 2 * i]] for i, pair in enumerate(moments)]


def solution(mesh):
    def step(x, dy, *arrays):
        weights, m, v = (arrays[i : i + 3] for i in (0, 3, 6))
        layers = weights[0].shape[0]
        assert layers == 2
        h0, by_y = x[0], dy[0]
        gate0, up0, act0, h1 = forward(h0, None, weights, 0)
        gate1, up1, by_down1, a_t = forward(h1, by_y, weights, 1)
        whole, new = backward(by_down1, [h0, h1, by_y, a_t], [gate1, up1, act0, gate0, up0], weights, list(zip(m, v)), 1)
        out = [jnp.stack([whole[ORDER.index((number, i))].reshape(weights[i].shape[1:]) for number in range(layers)]) for i in range(3)]
        return (*out, *(new[i][which] for which in (0, 1) for i in range(3)))

    blocks = P(None, "dp", None)
    return jax.shard_map(step, mesh=mesh, in_specs=(P(("rep", "dp")),) * 2 + (P(),) * 3 + (blocks,) * 6,
        out_specs=(P("rep"),) * 3 + (P("rep", "dp", None),) * 6, check_vma=False)
```

time: 2200 us -> 718 us (0.33)
  waiting for transfers between devices: 1740 us -> 0 us
  Pallas kernels: 0 us -> 656 us
  matrix products: 349 us -> 0 us
  local copies, waits for them, and re-layouts: 60.3 us -> 5.3 us
  other arithmetic: 29.3 us -> 55 us
    unnamed x15 -> x0, waiting for transfers between devices: 1340 us -> none
    pallas_call x0 -> x3, Pallas kernels: none -> 656 us  [the longest x1 558 us: backward(): pl.pallas_call(functools.partial(backward_kernel, (*away, *near)), in_spe...]
    reshape x3 -> x0, waiting for transfers between devices: 395 us -> none  [step(): t.reshape(-1, *t.shape[2:])]
    dot_general x15 -> x0, matrix products: 349 us -> none  [the longest x5 127 us: layer(): gate = jnp.dot(a, w['w_gate'], preferred_element_type=jnp.float32)]
    another operation x0 -> x2, other arithmetic: none -> 55 us  [step(): jnp.stack([whole[ORDER.index((number, i))].reshape(weights[i].shape[1:])...]
    unnamed x51 -> x18, local copies, waits for them, and re-layouts: 59.7 us -> 5.3 us
  transfers between devices with their start and end apart: 9 -> 0, of which waited for: 9 -> 0; matrix products, arithmetic and copies ran while one was open for 8% -> 0% of each run, Pallas kernels for 0% -> 0%
where the time goes in v3:
time: 718 us; the launch traced here: 717 us
  Pallas kernels  656 us (91%)
  other arithmetic  55 us (8%)
    pallas_call x1, Pallas kernels, backward(): pl.pallas_call(functools.partial(backward_kernel, (*away, *near)), in_spe...  558 us
    another operation x2, other arithmetic, step(): jnp.stack([whole[ORDER.index((number, i))].reshape(weights[i].shape[1:])...  55 us
    pallas_call x1, Pallas kernels, forward(): call(first_kernel, in_specs=[states, w_in, w_in, w_down], out_specs=[acro...  50.2 us
    pallas_call x1, Pallas kernels, forward(): call(last_kernel, in_specs=[states, states, w_in, w_in], out_specs=[acros...  48.3 us

profile of v3, /device:TPU:0, one launch (start us, length us, event | category | flops | bytes accessed | tf_op | source)
XLA Modules:
  0.0 717.4 jit_solution(12083619390907956252)
XLA Ops:
  0.6 50.2 %first.1 = (f32[1024,4096]{1,0:T(8,128)}, f32[1024,4096]{1,0:T(8,128)}, bf16[1024,4096]{1,0:T(8,128)(2,1)}, bf16[1024,1536]{1,0:T(8,128)(2,1)}) custom-call(bf16[1024,1536]{1,0:T(8,128)(2,1)} %bitcast.27, bf16[2,1536,4096]{2,1,0:T(8,128)(2,1)} %refs_0_.1, bf16[2,1536,4096]{2,1,0:T(8,128)(2,1)} %refs_1_.1, bf16[2,4096,1536]{2,1,0:T(8,128)(2,1)} %refs_2_.1), custom_call_target="tpu_custom_call" | custom-call | tf_op jit(solution)/shard_map/first/pallas_call | solution.py:403
  50.9 48.3 %last.1 = (f32[1024,4096]{1,0:T(8,128)}, f32[1024,4096]{1,0:T(8,128)}, bf16[64,3,8,4096]{3,2,1,0:T(8,128)(2,1)}, bf16[1536,1024]{1,0:T(8,128)(2,1)}) custom-call(bf16[1024,1536]{1,0:T(8,128)(2,1)} %get-tuple-element.29.h.h1, bf16[1024,1536]{1,0:T(8,128)(2,1)} %bitcast.29, bf16[2,1536,4096]{2,1,0:T(8,128)(2,1)} %refs_0_.1, bf16[2,1536,4096]{2,1,0:T(8,128)(2,1)} %refs_1_.1), custom_call_target="tpu_custom_call" | custom-call | tf_op jit(solution)/shard_map/last/pallas_call | solution.py:406
  99.1 557.9 %backward.1 = (bf16[4,4,4,8,8,1536]{5,4,3,2,1,0:T(8,128)(2,1)}, bf16[4,4,4,3,8,4096]{5,4,3,2,1,0:T(8,128)(2,1)}, bf16[4,4,4,3,8,4096]{5,4,3,2,1,0:T(8,128)(2,1)}...) custom-call(bf16[4,4,4,3,8,4096]{5,4,3,2,1,0:T(8,128)(2,1)} %bitcast, ...), custom_call_target="tpu_custom_call" | custom-call | tf_op jit(solution)/shard_map/backward/pallas_call | solution.py:629
  657.1 33.5 %pad_maximum_fusion = (bf16[2,1536,4096]{2,1,0:T(8,128)(2,1)}, bf16[2,1536,4096]{2,1,0:T(8,128)(2,1)}) fusion(bf16[1,1536,4096]{2,1,0:T(8,128)(2,1)} %bitcast.32, bf16[1,1536,4096]{2,1,0:T(8,128)(2,1)} %bitcast.34, bf16[1,1536,4096]{2,1,0:T(8,128)(2,1)} %bitcast.33, bf16[1,1536,4096]{2,1,0:T(8,128)(2,1)} %bitcast.35), kind=kLoop, calls=%fused_computation | loop fusion | flops 25165824 | bytes 100663296 | tf_op jit(solution)/shard_map/stack | solution.py:647
  690.6 0.0 copy-start.5
  690.6 0.0 copy-start.4
  690.6 0.0 copy-start.3
  690.6 0.0 copy-start.2
  690.6 0.0 copy-start.1
  690.6 0.0 copy-start
  690.7 21.5 %pad_maximum_fusion.2 = bf16[2,4096,1536]{2,1,0:T(8,128)(2,1)} fusion(bf16[1,4096,1536]{2,1,0:T(8,128)(2,1)} %bitcast.36, bf16[1,4096,1536]{2,1,0:T(8,128)(2,1)} %bitcast.37), kind=kLoop, calls=%fused_computation.2 | loop fusion | flops 12582912 | bytes 50331648 | tf_op jit(solution)/shard_map/stack | solution.py:647
  712.1 0.0 copy-done.5
  712.1 0.9 copy.26
  713.0 0.0 copy-done.4
  713.0 0.9 copy.27
  713.9 0.0 copy-done.3
  713.9 0.9 copy.28
  714.8 0.0 copy-done.2
  714.8 0.9 copy.29
  715.6 0.0 copy-done.1
  715.6 0.9 copy.30
  716.5 0.0 copy-done
  716.5 0.9 copy.31
Async XLA Ops:
  690.6 21.5 %copy-start.5 = (f32[2,3,8,4096]{3,2,1,0:T(8,128)S(1)}, f32[2,3,8,4096]{3,2,1,0:T(8,128)}, u32[]{:S(2)}) copy-start(f32[2,3,8,4096]{3,2,1,0:T(8,128)} %get-tuple-element.43) | copy-start | bytes 2359300
  690.6 22.4 %copy-start.4 = (f32[2,3,8,4096]{3,2,1,0:T(8,128)S(1)}, f32[2,3,8,4096]{3,2,1,0:T(8,128)}, u32[]{:S(2)}) copy-start(f32[2,3,8,4096]{3,2,1,0:T(8,128)} %get-tuple-element.44) | copy-start | bytes 2359300
  690.6 23.3 %copy-start.3 = (f32[2,8,8,1536]{3,2,1,0:T(8,128)S(1)}, f32[2,8,8,1536]{3,2,1,0:T(8,128)}, u32[]{:S(2)}) copy-start(f32[2,8,8,1536]{3,2,1,0:T(8,128)} %get-tuple-element.45) | copy-start | bytes 2359300
  690.6 24.1 %copy-start.2 = (f32[2,3,8,4096]{3,2,1,0:T(8,128)S(1)}, f32[2,3,8,4096]{3,2,1,0:T(8,128)}, u32[]{:S(2)}) copy-start(f32[2,3,8,4096]{3,2,1,0:T(8,128)} %get-tuple-element.46) | copy-start | bytes 2359300
  690.6 25.0 %copy-start.1 = (f32[2,3,8,4096]{3,2,1,0:T(8,128)S(1)}, f32[2,3,8,4096]{3,2,1,0:T(8,128)}, u32[]{:S(2)}) copy-start(f32[2,3,8,4096]{3,2,1,0:T(8,128)} %get-tuple-element.47) | copy-start | bytes 2359300
  690.6 25.9 %copy-start = (f32[2,8,8,1536]{3,2,1,0:T(8,128)S(1)}, f32[2,8,8,1536]{3,2,1,0:T(8,128)}, u32[]{:S(2)}) copy-start(f32[2,8,8,1536]{3,2,1,0:T(8,128)} %get-tuple-element.48) | copy-start | bytes 2359300
